TPU v7x, 32 devices: a whole 2x2x4 slice. The times are simulated.
32 devices in a mesh: mp: 2 (over core), tile: 16 (over z, y, x).
Axes of the slice: x: 2, y: 2, z: 4, core: 2. Of those that a mesh axis runs over, the one named last changes fastest.
Arguments:
- state: float32 [2, 20, 64, 1024], P('mp', None, 'tile'), may hold values from -6 to 6
- guess: float32 [2, 24, 64, 1024], P('mp', None, 'tile'), may hold values from -6 to 6
- regrid: bfloat16 [2, 16, 16, 256, 256], P('mp', 'tile'), may hold values from -1 to 1
- regime: int32 [2, 64, 1024], P('mp', 'tile'), may hold values from 0 to 3
- land: int32 [2, 64, 1024], P('mp', 'tile'), may hold values 0 or 1
- land_temp: float32 [2, 64, 1024], P('mp', 'tile'), may hold values from -6 to 6
- exchange_rate: float32 [2, 4], P('mp'), may hold values from 0.05 to 0.3
- vertical: float32 [2, 19], P('mp'), may hold values from 0.05 to 0.3
- mixing: float32 [2], P('mp'), may hold values from 0.02 to 0.1
Outputs:
- final_state: float32 [2, 20, 64, 1024], P('mp', None, 'tile')
- forcing: float32 [2, 24, 64, 1024], P('mp', None, 'tile')
All inputs are finite; a program needn't handle non-finite values. No bound on the sum of `land` on one device may be relied on, other than what follows from the above.
Results may differ from a plain program's by a relative error of at most 0.0029.
Values may be sent and summed in bfloat16 or wider, within the bound.
No kernel may reach another device: no remote copies, remote signals or barrier semaphores. Data moves between devices by JAX's collectives and lax.ppermute only.
A program may use at most 128 MiB of HBM per device.

v0:
```python
import jax
import jax.numpy as jnp
from jax import lax
from jax.sharding import PartitionSpec as P

ITERS = 2


def padded_2(array, sides, width):
    for axis, dim in sides:
        count, length = (lax.axis_size(axis), array.shape[dim])
        up = [(i, (i + 1) % count) for i in range(count - 1)]
        down = [(j, i) for i, j in up]
        last = lax.slice_in_dim(array, length - width, length, axis=dim)
        initial = lax.slice_in_dim(array, 0, width, axis=dim)
        before = lax.ppermute(last, axis, up)
        after = lax.ppermute(initial, axis, down)
        array = jnp.concatenate([before, array, after], axis=dim)
    return array


def from_partner(block, axis, bit):
    count = lax.axis_size(axis)
    route = []
    for low in range(count):
        high = low | 1 << bit
        if high != low and high < count:
            route += [(low, high), (high, low)]
    return lax.ppermute(block, axis, route)


def rate_field(regime, rates):
    field = jnp.zeros(regime.shape, jnp.float32)
    for kind_index in range(rates.shape[0]):
        field = field + jnp.where(
            regime == kind_index, rates[kind_index], jnp.zeros((), jnp.float32)
        )
    return field


def on_device(state, guess, regrid, regime, land, land_temp, exchange_rate, vertical, mixing):
    rows = state.shape[2]
    width = state.shape[3]
    steps = guess.shape[1]
    tiles = lax.axis_size("tile")
    face = width // tiles
    coeff = rate_field(regime[0], exchange_rate[0])
    land_local = land[0]
    land_value = land_temp[0]
    level_mix = vertical[0]
    surface_mix = mixing[0]
    blocks = regrid[0, 0].reshape(tiles, rows, face, rows, face)

    def one_step(carry, force_now):
        surface = carry[0]
        boundary = jnp.where(land_local == 1, land_value, force_now)
        flux = coeff * (boundary - surface)
        padded = padded_2(surface, (("tile", 0),), 1)
        lateral = (
            padded[2:]
            + padded[:-2]
            + jnp.roll(surface, 1, axis=1)
            + jnp.roll(surface, -1, axis=1)
            - 4.0 * surface
        )
        between = level_mix[:, None, None] * (carry[1:] - carry[:-1])
        change = jnp.pad(between, ((0, 1), (0, 0), (0, 0))) - jnp.pad(
            between, ((1, 0), (0, 0), (0, 0))
        )
        updated = carry + change
        updated = updated.at[0].add(flux + surface_mix * lateral)
        return (updated, updated[0].astype(jnp.bfloat16))

    forcing = guess[0]
    column = state[0]
    for sweep_index in range(ITERS):
        column, trace = lax.scan(one_step, state[0], forcing)
        shaped = trace.reshape(steps, rows, tiles, face)
        grouped = lax.all_to_all(shaped, "tile", split_axis=2, concat_axis=2, tiled=True)
        arrived = from_partner(grouped, "mp", 0)
        mapped = jnp.einsum("traw,apqrw->tpaq", arrived, blocks, preferred_element_type=jnp.float32)
        forcing = mapped.reshape(steps, rows, width)
    return (column[None], forcing[None])


def solution(mesh):
    return jax.shard_map(
        on_device,
        mesh=mesh,
        in_specs=(
            P("mp", None, "tile", None),
            P("mp", None, "tile", None),
            P("mp", "tile", None, None, None),
            P("mp", "tile", None),
            P("mp", "tile", None),
            P("mp", "tile", None),
            P("mp", None),
            P("mp", None),
            P("mp"),
        ),
        out_specs=(P("mp", None, "tile", None), P("mp", None, "tile", None)),
        check_vma=False,
    )
```

profile of v0, /device:TPU:0, one launch (start us, length us, event | category | flops | bytes accessed | tf_op | source)
XLA Modules:
  0.0 554.4 jit_solution(12810345093696615182)
XLA Ops:
  6.4 264.3 %while.30 = (s32[]{:T(128)}, f32[20,4,1024]{2,1,0:T(4,128)S(1)}, bf16[24,4,1024]{2,1,0:T(4,128)(2,1)S(1)}, f32[1,19]{1,0:T(1,128)}, s32[4,1024]{1,0:T(4,128)}, /...) while((s32[]{:T(128)}, f32[20,4,1024]{2,1,0:T(4,128)S(1)}, ...), condition=%wide.region_1.2_spmd, body=%wide.region_0.1_spmd.sunk | while | flops 389122 | bytes 2248977 | solution.py:77
  6.4 4.9 collective-permute-start
  18.3 4.3 collective-permute-start
  29.7 3.8 collective-permute-start
  40.5 4.8 collective-permute-start
  52.4 3.7 collective-permute-start
  63.1 4.0 collective-permute-start
  74.1 3.8 collective-permute-start
  85.0 4.8 collective-permute-start
  96.8 3.7 collective-permute-start
  107.6 4.0 collective-permute-start
  118.6 3.8 collective-permute-start
  129.4 4.8 collective-permute-start
  141.3 3.7 collective-permute-start
  152.1 4.0 collective-permute-start
  163.1 3.7 collective-permute-start
  173.8 3.7 collective-permute-start
  184.6 3.7 collective-permute-start
  195.4 3.7 collective-permute-start
  206.1 3.7 collective-permute-start
  216.9 3.7 collective-permute-start
  227.7 3.7 collective-permute-start
  238.4 3.7 collective-permute-start
  249.2 3.7 collective-permute-start
  260.0 3.7 collective-permute-start
  271.5 11.8 %all_to_all.10 = bf16[16,2,3072]{2,1,0:T(2,128)(2,1)S(1)} all-to-all(bf16[16,2,3072]{2,1,0:T(2,128)(2,1)S(1)} %reshape.149), channel_id=1, replica_groups=mesh['mp'=2,'tile'=16] {'tile'}, dimensions={0} | all-to-all | bytes 393216 | tf_op jit(solution)/shard_map/all_to_all | solution.py:79
  286.9 3.9 fusion.24
  291.7 242.6 %while.31 = (s32[]{:T(128)}, f32[20,4,1024]{2,1,0:T(4,128)S(1)}, bf16[24,4,1024]{2,1,0:T(4,128)(2,1)S(1)}, f32[1,19]{1,0:T(1,128)S(1)}, s32[4,1024]{1,0:T(4,128)...) while((s32[]{:T(128)}, f32[20,4,1024]{2,1,0:T(4,128)S(1)}, ...), condition=%wide.region_3.4_spmd, body=%wide.region_2.3_spmd.sunk | while | flops 389122 | bytes 2248977 | solution.py:77
  296.7 3.8 collective-permute-done.3
  301.3 3.7 collective-permute-start.2
  306.7 3.8 collective-permute-done.3
  311.3 3.7 collective-permute-start.2
  316.7 3.8 collective-permute-done.3
  321.3 4.8 collective-permute-start.2
  327.9 3.8 collective-permute-done.3
  337.9 3.8 collective-permute-done.3
  347.9 3.8 collective-permute-done.3
  352.4 3.7 collective-permute-start.2
  357.9 3.8 collective-permute-done.3
  362.5 4.4 collective-permute-start.2
  368.6 3.8 collective-permute-done.3
  378.6 3.8 collective-permute-done.3
  388.6 3.8 collective-permute-done.3
  398.6 3.8 collective-permute-done.3
  403.2 4.6 collective-permute-start.2
  409.6 3.8 collective-permute-done.3
  414.1 3.7 collective-permute-start.2
  419.6 3.8 collective-permute-done.3
  429.6 3.8 collective-permute-done.3
  434.2 3.7 collective-permute-start.2
  439.6 3.8 collective-permute-done.3
  449.6 3.8 collective-permute-done.3
  459.6 3.8 collective-permute-done.3
  469.6 3.8 collective-permute-done.3
  479.6 3.8 collective-permute-done.3
  489.7 3.8 collective-permute-done.3
  499.7 3.8 collective-permute-done.3
  504.2 3.7 collective-permute-start.2
  509.7 3.8 collective-permute-done.3
  519.7 3.8 collective-permute-done.3
  524.3 3.8 collective-permute-start.2
  529.8 3.8 collective-permute-done.3
  535.1 11.8 %all_to_all.11 = bf16[16,2,3072]{2,1,0:T(2,128)(2,1)S(1)} all-to-all(bf16[16,2,3072]{2,1,0:T(2,128)(2,1)S(1)} %reshape.151), channel_id=1, replica_groups=mesh['mp'=2,'tile'=16] {'tile'}, dimensions={0} | all-to-all | bytes 393216 | tf_op jit(solution)/shard_map/all_to_all | solution.py:79
  549.0 3.9 fusion.27
  (551 shorter events, 293.2 us)
Async XLA Ops:
  6.4 7.3 %collective-permute-start = (f32[1,1024]{1,0:T(1,128)S(1)}, f32[1,1024]{1,0:T(1,128)S(1)}, u32[]{:S(2)}, u32[]{:S(2)}) collective-permute-start(f32[1,1024]{1,0:T(1,128)S(1)} %get-tuple-element.446), channel_id=1, source_target_pairs={{0,1},{1,2},{2,3},{3,4},{4,5},{5,6},{6,7},{7,8},{8,9},{9,10},{10,1... | collective-permute-start | bytes 12296 | tf_op jit(solution)/shard_map/while/body/eval_jaxpr/ppermute | solution.py:16
  11.3 5.5 collective-permute-start.1
  18.3 6.7 %collective-permute-start = (f32[1,1024]{1,0:T(1,128)S(1)}, f32[1,1024]{1,0:T(1,128)S(1)}, u32[]{:S(2)}, u32[]{:S(2)}) collective-permute-start(f32[1,1024]{1,0:T(1,128)S(1)} %get-tuple-element.446), channel_id=1, source_target_pairs={{0,1},{1,2},{2,3},{3,4},{4,5},{5,6},{6,7},{7,8},{8,9},{9,10},{10,1... | collective-permute-start | bytes 12296 | tf_op jit(solution)/shard_map/while/body/eval_jaxpr/ppermute | solution.py:16
  22.6 5.5 collective-permute-start.1
  29.7 6.2 %collective-permute-start = (f32[1,1024]{1,0:T(1,128)S(1)}, f32[1,1024]{1,0:T(1,128)S(1)}, u32[]{:S(2)}, u32[]{:S(2)}) collective-permute-start(f32[1,1024]{1,0:T(1,128)S(1)} %get-tuple-element.446), channel_id=1, source_target_pairs={{0,1},{1,2},{2,3},{3,4},{4,5},{5,6},{6,7},{7,8},{8,9},{9,10},{10,1... | collective-permute-start | bytes 12296 | tf_op jit(solution)/shard_map/while/body/eval_jaxpr/ppermute | solution.py:16
  33.4 5.5 collective-permute-start.1
  40.5 7.2 %collective-permute-start = (f32[1,1024]{1,0:T(1,128)S(1)}, f32[1,1024]{1,0:T(1,128)S(1)}, u32[]{:S(2)}, u32[]{:S(2)}) collective-permute-start(f32[1,1024]{1,0:T(1,128)S(1)} %get-tuple-element.446), channel_id=1, source_target_pairs={{0,1},{1,2},{2,3},{3,4},{4,5},{5,6},{6,7},{7,8},{8,9},{9,10},{10,1... | collective-permute-start | bytes 12296 | tf_op jit(solution)/shard_map/while/body/eval_jaxpr/ppermute | solution.py:16
  45.3 5.5 collective-permute-start.1
  52.4 6.1 %collective-permute-start = (f32[1,1024]{1,0:T(1,128)S(1)}, f32[1,1024]{1,0:T(1,128)S(1)}, u32[]{:S(2)}, u32[]{:S(2)}) collective-permute-start(f32[1,1024]{1,0:T(1,128)S(1)} %get-tuple-element.446), channel_id=1, source_target_pairs={{0,1},{1,2},{2,3},{3,4},{4,5},{5,6},{6,7},{7,8},{8,9},{9,10},{10,1... | collective-permute-start | bytes 12296 | tf_op jit(solution)/shard_map/while/body/eval_jaxpr/ppermute | solution.py:16
  56.1 5.5 collective-permute-start.1
  63.1 6.4 %collective-permute-start = (f32[1,1024]{1,0:T(1,128)S(1)}, f32[1,1024]{1,0:T(1,128)S(1)}, u32[]{:S(2)}, u32[]{:S(2)}) collective-permute-start(f32[1,1024]{1,0:T(1,128)S(1)} %get-tuple-element.446), channel_id=1, source_target_pairs={{0,1},{1,2},{2,3},{3,4},{4,5},{5,6},{6,7},{7,8},{8,9},{9,10},{10,1... | collective-permute-start | bytes 12296 | tf_op jit(solution)/shard_map/while/body/eval_jaxpr/ppermute | solution.py:16
  67.1 5.5 collective-permute-start.1
  74.1 6.2 %collective-permute-start = (f32[1,1024]{1,0:T(1,128)S(1)}, f32[1,1024]{1,0:T(1,128)S(1)}, u32[]{:S(2)}, u32[]{:S(2)}) collective-permute-start(f32[1,1024]{1,0:T(1,128)S(1)} %get-tuple-element.446), channel_id=1, source_target_pairs={{0,1},{1,2},{2,3},{3,4},{4,5},{5,6},{6,7},{7,8},{8,9},{9,10},{10,1... | collective-permute-start | bytes 12296 | tf_op jit(solution)/shard_map/while/body/eval_jaxpr/ppermute | solution.py:16
  77.9 5.5 collective-permute-start.1
  85.0 7.2 %collective-permute-start = (f32[1,1024]{1,0:T(1,128)S(1)}, f32[1,1024]{1,0:T(1,128)S(1)}, u32[]{:S(2)}, u32[]{:S(2)}) collective-permute-start(f32[1,1024]{1,0:T(1,128)S(1)} %get-tuple-element.446), channel_id=1, source_target_pairs={{0,1},{1,2},{2,3},{3,4},{4,5},{5,6},{6,7},{7,8},{8,9},{9,10},{10,1... | collective-permute-start | bytes 12296 | tf_op jit(solution)/shard_map/while/body/eval_jaxpr/ppermute | solution.py:16
  89.8 5.5 collective-permute-start.1
  96.8 6.1 %collective-permute-start = (f32[1,1024]{1,0:T(1,128)S(1)}, f32[1,1024]{1,0:T(1,128)S(1)}, u32[]{:S(2)}, u32[]{:S(2)}) collective-permute-start(f32[1,1024]{1,0:T(1,128)S(1)} %get-tuple-element.446), channel_id=1, source_target_pairs={{0,1},{1,2},{2,3},{3,4},{4,5},{5,6},{6,7},{7,8},{8,9},{9,10},{10,1... | collective-permute-start | bytes 12296 | tf_op jit(solution)/shard_map/while/body/eval_jaxpr/ppermute | solution.py:16
  100.5 5.5 collective-permute-start.1
  107.6 6.4 %collective-permute-start = (f32[1,1024]{1,0:T(1,128)S(1)}, f32[1,1024]{1,0:T(1,128)S(1)}, u32[]{:S(2)}, u32[]{:S(2)}) collective-permute-start(f32[1,1024]{1,0:T(1,128)S(1)} %get-tuple-element.446), channel_id=1, source_target_pairs={{0,1},{1,2},{2,3},{3,4},{4,5},{5,6},{6,7},{7,8},{8,9},{9,10},{10,1... | collective-permute-start | bytes 12296 | tf_op jit(solution)/shard_map/while/body/eval_jaxpr/ppermute | solution.py:16
  111.6 5.5 collective-permute-start.1
  118.6 6.2 %collective-permute-start = (f32[1,1024]{1,0:T(1,128)S(1)}, f32[1,1024]{1,0:T(1,128)S(1)}, u32[]{:S(2)}, u32[]{:S(2)}) collective-permute-start(f32[1,1024]{1,0:T(1,128)S(1)} %get-tuple-element.446), channel_id=1, source_target_pairs={{0,1},{1,2},{2,3},{3,4},{4,5},{5,6},{6,7},{7,8},{8,9},{9,10},{10,1... | collective-permute-start | bytes 12296 | tf_op jit(solution)/shard_map/while/body/eval_jaxpr/ppermute | solution.py:16
  122.4 5.5 collective-permute-start.1
  129.4 7.2 %collective-permute-start = (f32[1,1024]{1,0:T(1,128)S(1)}, f32[1,1024]{1,0:T(1,128)S(1)}, u32[]{:S(2)}, u32[]{:S(2)}) collective-permute-start(f32[1,1024]{1,0:T(1,128)S(1)} %get-tuple-element.446), channel_id=1, source_target_pairs={{0,1},{1,2},{2,3},{3,4},{4,5},{5,6},{6,7},{7,8},{8,9},{9,10},{10,1... | collective-permute-start | bytes 12296 | tf_op jit(solution)/shard_map/while/body/eval_jaxpr/ppermute | solution.py:16
  134.3 5.5 collective-permute-start.1
  141.3 6.1 %collective-permute-start = (f32[1,1024]{1,0:T(1,128)S(1)}, f32[1,1024]{1,0:T(1,128)S(1)}, u32[]{:S(2)}, u32[]{:S(2)}) collective-permute-start(f32[1,1024]{1,0:T(1,128)S(1)} %get-tuple-element.446), channel_id=1, source_target_pairs={{0,1},{1,2},{2,3},{3,4},{4,5},{5,6},{6,7},{7,8},{8,9},{9,10},{10,1... | collective-permute-start | bytes 12296 | tf_op jit(solution)/shard_map/while/body/eval_jaxpr/ppermute | solution.py:16
  145.0 5.5 collective-permute-start.1
  152.1 6.4 %collective-permute-start = (f32[1,1024]{1,0:T(1,128)S(1)}, f32[1,1024]{1,0:T(1,128)S(1)}, u32[]{:S(2)}, u32[]{:S(2)}) collective-permute-start(f32[1,1024]{1,0:T(1,128)S(1)} %get-tuple-element.446), channel_id=1, source_target_pairs={{0,1},{1,2},{2,3},{3,4},{4,5},{5,6},{6,7},{7,8},{8,9},{9,10},{10,1... | collective-permute-start | bytes 12296 | tf_op jit(solution)/shard_map/while/body/eval_jaxpr/ppermute | solution.py:16
  156.0 5.5 collective-permute-start.1
  163.1 6.1 %collective-permute-start = (f32[1,1024]{1,0:T(1,128)S(1)}, f32[1,1024]{1,0:T(1,128)S(1)}, u32[]{:S(2)}, u32[]{:S(2)}) collective-permute-start(f32[1,1024]{1,0:T(1,128)S(1)} %get-tuple-element.446), channel_id=1, source_target_pairs={{0,1},{1,2},{2,3},{3,4},{4,5},{5,6},{6,7},{7,8},{8,9},{9,10},{10,1... | collective-permute-start | bytes 12296 | tf_op jit(solution)/shard_map/while/body/eval_jaxpr/ppermute | solution.py:16
  166.8 5.5 collective-permute-start.1
  173.8 6.1 %collective-permute-start = (f32[1,1024]{1,0:T(1,128)S(1)}, f32[1,1024]{1,0:T(1,128)S(1)}, u32[]{:S(2)}, u32[]{:S(2)}) collective-permute-start(f32[1,1024]{1,0:T(1,128)S(1)} %get-tuple-element.446), channel_id=1, source_target_pairs={{0,1},{1,2},{2,3},{3,4},{4,5},{5,6},{6,7},{7,8},{8,9},{9,10},{10,1... | collective-permute-start | bytes 12296 | tf_op jit(solution)/shard_map/while/body/eval_jaxpr/ppermute | solution.py:16
  177.6 5.5 collective-permute-start.1
  184.6 6.1 %collective-permute-start = (f32[1,1024]{1,0:T(1,128)S(1)}, f32[1,1024]{1,0:T(1,128)S(1)}, u32[]{:S(2)}, u32[]{:S(2)}) collective-permute-start(f32[1,1024]{1,0:T(1,128)S(1)} %get-tuple-element.446), channel_id=1, source_target_pairs={{0,1},{1,2},{2,3},{3,4},{4,5},{5,6},{6,7},{7,8},{8,9},{9,10},{10,1... | collective-permute-start | bytes 12296 | tf_op jit(solution)/shard_map/while/body/eval_jaxpr/ppermute | solution.py:16
  188.3 5.5 collective-permute-start.1
  195.4 6.1 %collective-permute-start = (f32[1,1024]{1,0:T(1,128)S(1)}, f32[1,1024]{1,0:T(1,128)S(1)}, u32[]{:S(2)}, u32[]{:S(2)}) collective-permute-start(f32[1,1024]{1,0:T(1,128)S(1)} %get-tuple-element.446), channel_id=1, source_target_pairs={{0,1},{1,2},{2,3},{3,4},{4,5},{5,6},{6,7},{7,8},{8,9},{9,10},{10,1... | collective-permute-start | bytes 12296 | tf_op jit(solution)/shard_map/while/body/eval_jaxpr/ppermute | solution.py:16
  199.1 5.5 collective-permute-start.1
  206.1 6.1 %collective-permute-start = (f32[1,1024]{1,0:T(1,128)S(1)}, f32[1,1024]{1,0:T(1,128)S(1)}, u32[]{:S(2)}, u32[]{:S(2)}) collective-permute-start(f32[1,1024]{1,0:T(1,128)S(1)} %get-tuple-element.446), channel_id=1, source_target_pairs={{0,1},{1,2},{2,3},{3,4},{4,5},{5,6},{6,7},{7,8},{8,9},{9,10},{10,1... | collective-permute-start | bytes 12296 | tf_op jit(solution)/shard_map/while/body/eval_jaxpr/ppermute | solution.py:16
  209.9 5.5 collective-permute-start.1
  216.9 6.1 %collective-permute-start = (f32[1,1024]{1,0:T(1,128)S(1)}, f32[1,1024]{1,0:T(1,128)S(1)}, u32[]{:S(2)}, u32[]{:S(2)}) collective-permute-start(f32[1,1024]{1,0:T(1,128)S(1)} %get-tuple-element.446), channel_id=1, source_target_pairs={{0,1},{1,2},{2,3},{3,4},{4,5},{5,6},{6,7},{7,8},{8,9},{9,10},{10,1... | collective-permute-start | bytes 12296 | tf_op jit(solution)/shard_map/while/body/eval_jaxpr/ppermute | solution.py:16
  220.6 5.5 collective-permute-start.1
  227.7 6.1 %collective-permute-start = (f32[1,1024]{1,0:T(1,128)S(1)}, f32[1,1024]{1,0:T(1,128)S(1)}, u32[]{:S(2)}, u32[]{:S(2)}) collective-permute-start(f32[1,1024]{1,0:T(1,128)S(1)} %get-tuple-element.446), channel_id=1, source_target_pairs={{0,1},{1,2},{2,3},{3,4},{4,5},{5,6},{6,7},{7,8},{8,9},{9,10},{10,1... | collective-permute-start | bytes 12296 | tf_op jit(solution)/shard_map/while/body/eval_jaxpr/ppermute | solution.py:16
  231.4 5.5 collective-permute-start.1
  238.4 6.1 %collective-permute-start = (f32[1,1024]{1,0:T(1,128)S(1)}, f32[1,1024]{1,0:T(1,128)S(1)}, u32[]{:S(2)}, u32[]{:S(2)}) collective-permute-start(f32[1,1024]{1,0:T(1,128)S(1)} %get-tuple-element.446), channel_id=1, source_target_pairs={{0,1},{1,2},{2,3},{3,4},{4,5},{5,6},{6,7},{7,8},{8,9},{9,10},{10,1... | collective-permute-start | bytes 12296 | tf_op jit(solution)/shard_map/while/body/eval_jaxpr/ppermute | solution.py:16
  242.2 5.5 collective-permute-start.1
  249.2 6.1 %collective-permute-start = (f32[1,1024]{1,0:T(1,128)S(1)}, f32[1,1024]{1,0:T(1,128)S(1)}, u32[]{:S(2)}, u32[]{:S(2)}) collective-permute-start(f32[1,1024]{1,0:T(1,128)S(1)} %get-tuple-element.446), channel_id=1, source_target_pairs={{0,1},{1,2},{2,3},{3,4},{4,5},{5,6},{6,7},{7,8},{8,9},{9,10},{10,1... | collective-permute-start | bytes 12296 | tf_op jit(solution)/shard_map/while/body/eval_jaxpr/ppermute | solution.py:16
  252.9 5.5 collective-permute-start.1
  260.0 6.1 %collective-permute-start = (f32[1,1024]{1,0:T(1,128)S(1)}, f32[1,1024]{1,0:T(1,128)S(1)}, u32[]{:S(2)}, u32[]{:S(2)}) collective-permute-start(f32[1,1024]{1,0:T(1,128)S(1)} %get-tuple-element.446), channel_id=1, source_target_pairs={{0,1},{1,2},{2,3},{3,4},{4,5},{5,6},{6,7},{7,8},{8,9},{9,10},{10,1... | collective-permute-start | bytes 12296 | tf_op jit(solution)/shard_map/while/body/eval_jaxpr/ppermute | solution.py:16
  263.7 5.5 collective-permute-start.1
  295.0 5.5 collective-permute-start.3
  315.0 5.5 collective-permute-start.3
  321.3 6.5 %collective-permute-start.2 = (f32[1,1024]{1,0:T(1,128)S(1)}, f32[1,1024]{1,0:T(1,128)S(1)}, u32[]{:S(2)}, u32[]{:S(2)}) collective-permute-start(f32[1,1024]{1,0:T(1,128)S(1)} %get-tuple-element.463), channel_id=1, source_target_pairs={{0,1},{1,2},{2,3},{3,4},{4,5},{5,6},{6,7},{7,8},{8,9},{9,10},{10,1... | collective-permute-start | bytes 12296 | tf_op jit(solution)/shard_map/while/body/eval_jaxpr/ppermute | solution.py:16
  326.1 5.5 collective-permute-start.3
  336.1 5.5 collective-permute-start.3
  356.2 5.5 collective-permute-start.3
  362.5 6.1 %collective-permute-start.2 = (f32[1,1024]{1,0:T(1,128)S(1)}, f32[1,1024]{1,0:T(1,128)S(1)}, u32[]{:S(2)}, u32[]{:S(2)}) collective-permute-start(f32[1,1024]{1,0:T(1,128)S(1)} %get-tuple-element.463), channel_id=1, source_target_pairs={{0,1},{1,2},{2,3},{3,4},{4,5},{5,6},{6,7},{7,8},{8,9},{9,10},{10,1... | collective-permute-start | bytes 12296 | tf_op jit(solution)/shard_map/while/body/eval_jaxpr/ppermute | solution.py:16
  376.9 5.5 collective-permute-start.3
  386.9 5.5 collective-permute-start.3
  403.2 6.4 %collective-permute-start.2 = (f32[1,1024]{1,0:T(1,128)S(1)}, f32[1,1024]{1,0:T(1,128)S(1)}, u32[]{:S(2)}, u32[]{:S(2)}) collective-permute-start(f32[1,1024]{1,0:T(1,128)S(1)} %get-tuple-element.463), channel_id=1, source_target_pairs={{0,1},{1,2},{2,3},{3,4},{4,5},{5,6},{6,7},{7,8},{8,9},{9,10},{10,1... | collective-permute-start | bytes 12296 | tf_op jit(solution)/shard_map/while/body/eval_jaxpr/ppermute | solution.py:16
  427.9 5.5 collective-permute-start.3
  457.9 5.5 collective-permute-start.3
  477.9 5.5 collective-permute-start.3
  487.9 5.5 collective-permute-start.3
  508.0 5.5 collective-permute-start.3
  518.0 5.5 collective-permute-start.3
  (39 other events, 226.0 us)
where the time goes:
time: 562 us; the launch traced here: 554 us
  starting transfers between devices  249 us (44%)
  waiting for transfers between devices  168 us (30%)
  other arithmetic  84.5 us (15%)
  blocking collectives  23.5 us (4%)
  local copies, waits for them, and re-layouts  18.3 us (3%)
  matrix products  7.85 us (1%)
    ppermute x48, starting transfers between devices, padded_2(): before = lax.ppermute(last, axis, up)  187 us
    ppermute x48, waiting for transfers between devices, padded_2(): after = lax.ppermute(initial, axis, down)  166 us
    ppermute x48, starting transfers between devices, padded_2(): after = lax.ppermute(initial, axis, down)  62 us
    dynamic_update_slice x48, other arithmetic, on_device(): column, trace = lax.scan(one_step, state[0], forcing)  53.7 us
    all_to_all x2, blocking collectives, on_device(): lax.all_to_all(shaped, 'tile', split_axis=2, concat_axis=2, tiled=True)  23.5 us
    mul x48, other arithmetic, one_step(): between = level_mix[:, None, None] * (carry[1:] - carry[:-1])  21.4 us
  transfers between devices with their start and end apart: 98, of which 49 were waited for; matrix products, arithmetic and copies ran while one was open for 7% of the time, Pallas kernels for 0%

commit v1 on v0

v1 whole, which is shorter than its diff:
```python
import functools

import jax
import jax.numpy as jnp
from jax import lax
from jax.experimental import pallas as pl
from jax.experimental.pallas import tpu as pltpu
from jax.sharding import PartitionSpec as P

ITERS = 2
LANES = 128
SUBLANES = 8
EXACT = lax.Precision.HIGHEST
SMEM = pl.BlockSpec(memory_space=pltpu.SMEM)
VMEM = pl.BlockSpec(memory_space=pltpu.VMEM)


def lane_of(shape):
    return lax.broadcasted_iota(jnp.int32, shape, len(shape) - 1)


def row_of(shape):
    return lax.broadcasted_iota(jnp.int32, shape, 0)


def tiles_of(width):
    return [pl.ds(k * LANES, LANES) for k in range(width // LANES)]


def windows(tile, count, face):
    half = (LANES - face) // 2
    for k in range(count):
        own, left, right = tile(k), tile((k - 1) % count), tile((k + 1) % count)
        lane = lane_of(own.shape)
        yield 2 * k, jnp.where(lane < face + half, own, left)
        yield 2 * k + 1, pltpu.roll(jnp.where(lane < half, right, own), face, axis=1)


def joined(first, second, face):
    out = []
    for j in range(first.shape[1] // LANES):
        cut = slice(j * LANES, (j + 1) * LANES)
        x, y = first[:, cut], second[:, cut]
        lane = lane_of(x.shape)
        out.append(jnp.where(lane < face, x, pltpu.roll(y, face, axis=1)))
        out.append(jnp.where(lane < face, pltpu.roll(x, face, axis=1), y))
    return out


def prepare(rates, vertical, state, guess, regime, land, land_temp, chunk, base, sea, mats, memory, xs, by_row, levels):
    lev, rows, width = state.shape
    steps = guess.shape[0]
    padded = xs.shape[0] // (steps + 1)
    face = width // chunk.shape[0]

    shape = (padded, LANES)
    row, lane = row_of(shape), lane_of(shape)
    up = jnp.zeros(shape, jnp.float32)
    down = jnp.zeros(shape, jnp.float32)
    for l in range(lev - 1):
        up = jnp.where((row == l) & (row > 0), vertical[0, l], up)
        down = jnp.where(row == l + 1, vertical[0, l], down)
    keep = jnp.where(row == 0, 0.0, 1.0 - up - down)
    power = jnp.where((row == lane) & (row < lev), 1.0, 0.0)
    answer = jnp.zeros(shape, jnp.float32)
    for n in range(steps + 1):
        xs[pl.ds(n * padded, padded), :] = power
        if n == steps:
            break
        answer = jnp.where(lane == steps - 1 - n, power[:, 0:1], answer)
        power = keep * power + up * pltpu.roll(power, padded - 1, axis=0) + down * pltpu.roll(power, 1, axis=0)
    mats[0] = jnp.where(row == 0, 0.0, power)
    mats[1] = answer
    first = xs[pl.ds(1, steps, stride=padded), :]
    v0 = vertical[0, 0]
    memory[...] = jnp.broadcast_to(v0 * first[:, 0:1], first.shape)
    to_below = jnp.where(lane_of(first.shape) == 0, 0.0, v0 * first)[:, :padded]

    coeff = jnp.zeros(regime.shape, jnp.float32)
    for kind in range(rates.shape[1]):
        coeff = jnp.where(regime[...] == kind, rates[0, kind], coeff)
    on_land = land[...] == 1
    sea[...] = jnp.where(on_land, 0.0, coeff)
    fixed = jnp.where(on_land, coeff * land_temp[...], 0.0)

    count = width // LANES
    rest = pl.ds(lev * rows, (padded - lev) * rows)
    for k, cut in enumerate(tiles_of(width)):
        for l in range(lev):
            levels[k, pl.ds(l * rows, rows), :] = state[l, :, cut]
        levels[k, rest, :] = jnp.zeros((rest.size, LANES), jnp.float32)
        for t in range(steps):
            by_row[k, pl.ds(t * rows, rows), :] = guess[t, :, cut]
    for p in range(rows):
        drives = []
        for k, cut in enumerate(tiles_of(width)):
            own = levels[k, pl.ds(p, padded, stride=rows), :]
            below = jnp.dot(to_below, own, precision=EXACT, preferred_element_type=jnp.float32)
            part = below + fixed[p : p + 1, k * LANES : (k + 1) * LANES]
            base[p, :, cut] = part
            drives.append(part + sea[p : p + 1, cut] * by_row[k, pl.ds(p, steps, stride=rows), :])
        for a, window in windows(lambda k: drives[k], count, face):
            chunk[a, pl.ds(p * steps, steps), :] = window.astype(jnp.bfloat16)
    fields = jnp.concatenate([state[0], regime[...].astype(jnp.float32)], axis=0)
    for a, window in windows(lambda k: fields[:, k * LANES : (k + 1) * LANES], count, face):
        chunk[a, pl.ds(rows * steps, 2 * rows), :] = window.astype(jnp.bfloat16)


def evolve(first, rates, vertical, mixing, memory, arrived, *refs):
    if first:
        fields, trace, drive, past, packed = refs
    else:
        fields, trace, drive, past, packed = refs
    tiles, steps, cells = trace.shape
    grid_rows = fields.shape[1]
    rows = grid_rows // tiles
    face = cells // rows
    held = rows * steps
    for a in range(tiles):
        drive[pl.ds(a * held, held), :] = arrived[a, pl.ds(0, held), :].astype(jnp.float32)
    side = pl.ds(SUBLANES, grid_rows)
    if first:
        for a in range(tiles):
            both = arrived[a, pl.ds(held, 2 * rows), :].astype(jnp.float32)
            fields[0, pl.ds(a * rows, rows), :] = both[:rows]
            fields[1, pl.ds(a * rows, rows), :] = both[rows:]
        regime = fields[1]
        coeff = jnp.zeros(regime.shape, jnp.float32)
        for kind in range(rates.shape[1]):
            coeff = jnp.where(regime == kind, rates[0, kind], coeff)
        fields[1] = 1.0 - vertical[0, 0] - coeff - 4.0 * mixing[0]
    stay = fields[1]
    mix = mixing[0]
    edge = jnp.zeros((SUBLANES, LANES), jnp.float32)
    for n in range(steps + 1):
        past[n, pl.ds(0, SUBLANES), :] = edge
        past[n, pl.ds(SUBLANES + grid_rows, SUBLANES), :] = edge
    surface = fields[0]
    past[0, side, :] = surface
    lane = lane_of((tiles, LANES))
    for n in range(steps):
        known = drive[pl.ds(n, grid_rows, stride=steps), :]
        for k in range(n):
            known = known + memory[n - k : n - k + 1, :] * past[k, side, :]
        lateral = past[n, pl.ds(SUBLANES - 1, grid_rows), :] + past[n, pl.ds(SUBLANES + 1, grid_rows), :]
        lateral = lateral + (pltpu.roll(surface, 1, axis=1) + pltpu.roll(surface, LANES - 1, axis=1))
        surface = (stay * surface + known) + mix * lateral
        past[n + 1, side, :] = surface
        for j in range(cells // LANES):
            even = past[n + 1, pl.ds(SUBLANES + 2 * j, tiles, stride=rows), :]
            odd = past[n + 1, pl.ds(SUBLANES + 2 * j + 1, tiles, stride=rows), :]
            packed[j, pl.ds(n, tiles, stride=steps), :] = jnp.where(lane < face, even, pltpu.roll(odd, face, axis=1))
    for j in range(cells // LANES):
        for a in range(tiles):
            trace[a, :, pl.ds(j * LANES, LANES)] = packed[j, pl.ds(a * steps, steps), :].astype(jnp.bfloat16)


def product(trace, regrid, a):
    return lax.dot_general(trace[a], regrid[a], (((1,), (1,)), ((), ())), preferred_element_type=jnp.float32)


def redrive(trace, regrid, base, sea, chunk, drive):
    tiles, steps, cells = trace.shape
    rows, _, width = base.shape
    face = cells // rows
    count = width // LANES
    for k, cut in enumerate(tiles_of(width)):
        mapped = joined(product(trace, regrid, 2 * k), product(trace, regrid, 2 * k + 1), face)
        for p in range(rows):
            drive[p, :, cut] = base[p, :, cut] + sea[p : p + 1, cut] * mapped[p]
    for p in range(rows):
        for a, window in windows(lambda k: drive[p, :, k * LANES : (k + 1) * LANES], count, face):
            chunk[a, pl.ds(p * steps, steps), :] = window.astype(jnp.bfloat16)


def remap(trace, regrid, forcing, by_row):
    tiles, steps, cells = trace.shape
    _, rows, width = forcing.shape
    face = cells // rows
    for k, cut in enumerate(tiles_of(width)):
        mapped = joined(product(trace, regrid, 2 * k), product(trace, regrid, 2 * k + 1), face)
        for p in range(rows):
            by_row[k, pl.ds(p, steps, stride=rows), :] = mapped[p]
        for t in range(steps):
            forcing[t, :, cut] = by_row[k, pl.ds(t * rows, rows), :]


def finish(history, state, mats, final, levels, by_row):
    tiles, steps, cells = history.shape
    lev, rows, width = state.shape
    padded = levels.shape[1] // rows
    face = cells // rows
    rest = pl.ds(lev * rows, (padded - lev) * rows)
    still = mats[0][:, :padded]
    answer = mats[1][:, :steps]
    for k, cut in enumerate(tiles_of(width)):
        for l in range(lev):
            levels[k, pl.ds(l * rows, rows), :] = state[l, :, cut]
        levels[k, rest, :] = jnp.zeros((rest.size, LANES), jnp.float32)
        seen = joined(history[2 * k].astype(jnp.float32), history[2 * k + 1].astype(jnp.float32), face)
        for p in range(rows):
            own = levels[k, pl.ds(p, padded, stride=rows), :]
            end = jnp.dot(still, own, precision=EXACT, preferred_element_type=jnp.float32)
            end = end + jnp.dot(answer, seen[p], precision=EXACT, preferred_element_type=jnp.float32)
            by_row[k, pl.ds(p, padded, stride=rows), :] = end
        for l in range(lev):
            final[l, :, cut] = by_row[k, pl.ds(l * rows, rows), :]


def on_device(state, guess, regrid, regime, land, land_temp, exchange_rate, vertical, mixing):
    _, lev, rows, width = state.shape
    steps = guess.shape[1]
    tiles = lax.axis_size("tile")
    face = width // tiles
    cells = rows * face
    grid_rows = rows * tiles
    if 2 * face != LANES or LANES - face < 2 * steps or (2 * rows) % SUBLANES or steps % SUBLANES:
        raise ValueError("unsupported sizes")
    padded = -(-lev // SUBLANES) * SUBLANES
    f32, bf16 = jnp.float32, jnp.bfloat16
    shape = jax.ShapeDtypeStruct
    state, guess, blocks = state[0], guess[0], regrid[0, 0]

    chunk, base, sea, mats, memory = pl.pallas_call(
        prepare,
        out_shape=(
            shape((tiles, rows * steps + 2 * rows, LANES), bf16),
            shape((rows, steps, width), f32),
            shape((rows, width), f32),
            shape((2, padded, LANES), f32),
            shape((steps, LANES), f32),
        ),
        in_specs=[SMEM, SMEM] + [VMEM] * 5,
        out_specs=(VMEM,) * 5,
        scratch_shapes=[
            pltpu.VMEM(((steps + 1) * padded, LANES), f32),
            pltpu.VMEM((width // LANES, steps * rows, LANES), f32),
            pltpu.VMEM((width // LANES, padded * rows, LANES), f32),
        ],
        name="prepare",
    )(exchange_rate, vertical, state, guess, regime[0], land[0], land_temp[0])

    fields = None
    for sweep in range(ITERS):
        arrived = lax.all_to_all(chunk, "tile", split_axis=0, concat_axis=0, tiled=True)
        trace_shape = shape((tiles, steps, cells), bf16)
        fields_shape = shape((2, grid_rows, LANES), f32)
        first = fields is None
        got = pl.pallas_call(
            functools.partial(evolve, first),
            out_shape=(fields_shape, trace_shape) if first else trace_shape,
            in_specs=[SMEM] * 3 + [VMEM] * (2 if first else 3),
            out_specs=(VMEM, VMEM) if first else VMEM,
            scratch_shapes=[
                pltpu.VMEM((tiles * rows * steps, LANES), f32),
                pltpu.VMEM((steps + 1, grid_rows + 2 * SUBLANES, LANES), f32),
                pltpu.VMEM((cells // LANES, tiles * steps, LANES), f32),
            ],
            name="evolve",
        )(exchange_rate, vertical, mixing, memory, arrived, *(() if first else (fields,)))
        fields, trace = got if first else (fields, got)
        partner = lax.ppermute(trace, "mp", [(0, 1), (1, 0)])
        if sweep < ITERS - 1:
            chunk = pl.pallas_call(
                redrive,
                out_shape=shape((tiles, rows * steps, LANES), bf16),
                in_specs=[VMEM] * 4,
                out_specs=VMEM,
                scratch_shapes=[pltpu.VMEM((rows, steps, width), f32)],
                name="redrive",
            )(partner, blocks, base, sea)
    forcing = pl.pallas_call(
        remap,
        out_shape=shape((steps, rows, width), f32),
        in_specs=[VMEM] * 2,
        out_specs=VMEM,
        scratch_shapes=[pltpu.VMEM((width // LANES, steps * rows, LANES), f32)],
        name="remap",
    )(partner, blocks)
    history = lax.all_to_all(trace, "tile", split_axis=0, concat_axis=0, tiled=True)
    final = pl.pallas_call(
        finish,
        out_shape=shape((lev, rows, width), f32),
        in_specs=[VMEM] * 3,
        out_specs=VMEM,
        scratch_shapes=[pltpu.VMEM((width // LANES, padded * rows, LANES), f32)] * 2,
        name="finish",
    )(history, state, mats)
    return final[None], forcing[None]


def solution(mesh):
    return jax.shard_map(
        on_device,
        mesh=mesh,
        in_specs=(
            P("mp", None, "tile", None),
            P("mp", None, "tile", None),
            P("mp", "tile", None, None, None),
            P("mp", "tile", None),
            P("mp", "tile", None),
            P("mp", "tile", None),
            P("mp", None),
            P("mp", None),
            P("mp"),
        ),
        out_specs=(P("mp", None, "tile", None), P("mp", None, "tile", None)),
        check_vma=False,
    )
```

time: 562 us -> 73.1 us (0.13); the launches traced: 554 us -> 72.5 us
  starting transfers between devices: 249 us -> 12 us
  waiting for transfers between devices: 168 us -> 18.3 us
  other arithmetic: 84.5 us -> 0 us
  Pallas kernels: 0 us -> 20.8 us
  local copies, waits for them, and re-layouts: 18.3 us -> 2.78 us
  matrix products: 7.85 us -> 0 us
  blocking collectives: 23.5 us -> 17.4 us
    ppermute x98 -> x2, starting transfers between devices: 249 us -> 0.07 us  [on_device(): partner = lax.ppermute(trace, 'mp', [(0, 1), (1, 0)])]
    ppermute x98 -> x2, waiting for transfers between devices: 168 us -> 3.29 us  [on_device(): partner = lax.ppermute(trace, 'mp', [(0, 1), (1, 0)])]
    dynamic_update_slice x48 -> x0, other arithmetic: 53.7 us -> none  [on_device(): column, trace = lax.scan(one_step, state[0], forcing)]
    mul x48 -> x0, other arithmetic: 21.4 us -> none  [one_step(): between = level_mix[:, None, None] * (carry[1:] - carry[:-1])]
    pallas_call x0 -> x6, Pallas kernels: none -> 20.8 us  [the longest x2 7.59 us: on_device(): pl.pallas_call(functools.partial(evolve, first), out_shape=(fields_shape,...]
    all_to_all x0 -> x2, waiting for transfers between devices: none -> 15 us  [the longest x1 12.6 us: on_device(): lax.all_to_all(chunk, 'tile', split_axis=0, concat_axis=0, tiled=True)]
    all_to_all x0 -> x2, starting transfers between devices: none -> 11.9 us  [the longest x1 8.33 us: on_device(): lax.all_to_all(chunk, 'tile', split_axis=0, concat_axis=0, tiled=True)]
    add x49 -> x0, other arithmetic: 9.39 us -> none  [the longest x48 6.16 us: one_step(): updated = carry + change]
  transfers between devices with their start and end apart: 98 -> 4, of which waited for: 49 -> 4; matrix products, arithmetic and copies ran while one was open for 7% -> 0% of each run, Pallas kernels for 0% -> 5%
where the time goes in v1:
time: 73.1 us; the launch traced here: 72.5 us
  Pallas kernels  20.8 us (28%)
  waiting for transfers between devices  18.3 us (25%)
  blocking collectives  17.4 us (24%)
  starting transfers between devices  12 us (16%)
  local copies, waits for them, and re-layouts  2.78 us (4%)
  between operations  1.31 us (2%)
    all_to_all x1, blocking collectives, on_device(): lax.all_to_all(chunk, 'tile', split_axis=0, concat_axis=0, tiled=True)  17.4 us
    all_to_all x1, waiting for transfers between devices, on_device(): lax.all_to_all(chunk, 'tile', split_axis=0, concat_axis=0, tiled=True)  12.6 us
    all_to_all x1, starting transfers between devices, on_device(): lax.all_to_all(chunk, 'tile', split_axis=0, concat_axis=0, tiled=True)  8.33 us
    pallas_call x2, Pallas kernels, on_device(): pl.pallas_call(functools.partial(evolve, first), out_shape=(fields_shape,...  7.59 us
    all_to_all x1, starting transfers between devices, on_device(): lax.all_to_all(trace, 'tile', split_axis=0, concat_axis=0, tiled=True)  3.59 us
    pallas_call x1, Pallas kernels, on_device(): pl.pallas_call(finish, out_shape=shape((lev, rows, width), f32), in_specs...  3.55 us
    pallas_call x1, Pallas kernels, on_device(): pl.pallas_call(redrive, out_shape=shape((tiles, rows * steps, LANES), bf1...  3.31 us
    pallas_call x1, Pallas kernels, on_device(): pl.pallas_call(remap, out_shape=shape((steps, rows, width), f32), in_spec...  3.3 us
  transfers between devices with their start and end apart: 4, of which 4 were waited for; matrix products, arithmetic and copies ran while one was open for 0% of the time, Pallas kernels for 5%

profile of v1, /device:TPU:0, one launch (start us, length us, event | category | flops | bytes accessed | tf_op | source)
XLA Modules:
  0.0 72.5 jit_solution(10176058306073993070)
XLA Ops:
  0.6 3.0 %prepare.1 = (bf16[16,104,128]{2,1,0:T(8,128)(2,1)}, f32[4,24,1024]{2,1,0:T(8,128)}, f32[4,1024]{1,0:T(4,128)}, f32[2,24,128]{2,1,0:T(8,128)}, f32[24,128]{1,0:T(8,128)}) custom-call(f32[1,4]{1,0:T(1,128)} %rates.5, f32[1,19]{1,0:T(1,128)} %vertical.5, f32[20,4,1024]{2,1,0:T(4,128)} %bitcast.10, f32[24,4,1024]{2,1,0:T(4,128)} %bitcast.12, ...), custom_call_target="tpu_custom_call" | custom-call | tf_op jit(solution)/shard_map/prepare/pallas_call | solution.py:224
  3.7 8.3 %all-to-all-start = ((bf16[16,104,128]{2,1,0:T(8,128)(2,1)}), bf16[16,104,128]{2,1,0:T(8,128)(2,1)S(1)}, u32[]{:S(2)}, u32[]{:S(2)}) async-start(bf16[16,104,128]{2,1,0:T(8,128)(2,1)} %get-tuple-element.10), calls=%async_computation | async-start | bytes 851968 | tf_op jit(solution)/shard_map/all_to_all | solution.py:245
  12.7 12.6 %all-to-all-done.arrived = bf16[16,104,128]{2,1,0:T(8,128)(2,1)S(1)} async-done(((bf16[16,104,128]{2,1,0:T(8,128)(2,1)}), bf16[16,104,128]{2,1,0:T(8,128)(2,1)S(1)}, u32[]{:S(2)}, u32[]{:S(2)}) %all-to-all-start) | async-done | bytes 426016 | tf_op jit(solution)/shard_map/all_to_all | solution.py:245
  25.3 0.0 copy-start
  25.3 0.8 %copy-done = bf16[16,104,128]{2,1,0:T(8,128)(2,1)} copy-done((bf16[16,104,128]{2,1,0:T(8,128)(2,1)}, bf16[16,104,128]{2,1,0:T(8,128)(2,1)S(1)}, u32[]{:S(2)}) %copy-start) | copy-done | bytes 426008
  26.0 3.8 %evolve.2 = (f32[2,64,128]{2,1,0:T(8,128)}, bf16[16,24,256]{2,1,0:T(8,128)(2,1)}) custom-call(f32[1,4]{1,0:T(1,128)} %rates.5, f32[1,19]{1,0:T(1,128)} %vertical.5, f32[1]{0:T(128)S(6)} %copy.11.mixing, f32[24,128]{1,0:T(8,128)} %get-tuple-element.9.memory, bf16[16,104,128]{2,1,0:T(8,128)(2,1)} %copy-done), custom_call_target="tpu_custom_call" | custom-call | tf_op jit(solution)/shard_map/evolve/pallas_call | solution.py:249
  29.8 0.0 collective-permute-start
  29.8 1.6 %collective-permute-done.trace = bf16[16,24,256]{2,1,0:T(8,128)(2,1)S(1)} collective-permute-done((bf16[16,24,256]{2,1,0:T(8,128)(2,1)}, bf16[16,24,256]{2,1,0:T(8,128)(2,1)S(1)}, u32[]{:S(2)}, u32[]{:S(2)}) %collective-permute-start) | collective-permute-done | bytes 196640 | tf_op jit(solution)/shard_map/ppermute | solution.py:262
  31.5 0.0 copy-start.2
  31.5 0.7 copy-done.2
  32.1 3.3 %redrive.1 = bf16[16,96,128]{2,1,0:T(8,128)(2,1)} custom-call(bf16[16,24,256]{2,1,0:T(8,128)(2,1)} %copy-done.2, bf16[16,256,256]{2,1,0:T(8,128)(2,1)} %bitcast.8, f32[4,24,1024]{2,1,0:T(8,128)} %get-tuple-element.12.base, f32[4,1024]{1,0:T(4,128)} %get-tuple-element.13.sea), custom_call_target="tpu_custom_call" | custom-call | tf_op jit(solution)/shard_map/redrive/pallas_call | solution.py:264
  35.5 17.4 %all_to_all.15.arrived = bf16[16,96,128]{2,1,0:T(8,128)(2,1)} all-to-all(bf16[16,96,128]{2,1,0:T(8,128)(2,1)} %redrive.1), channel_id=1, replica_groups=mesh['mp'=2,'tile'=16] {'tile'}, dimensions={0} | all-to-all | bytes 786432 | tf_op jit(solution)/shard_map/all_to_all | solution.py:245
  52.8 3.8 %evolve.3 = bf16[16,24,256]{2,1,0:T(8,128)(2,1)} custom-call(f32[1,4]{1,0:T(1,128)} %rates.5, f32[1,19]{1,0:T(1,128)} %vertical.5, f32[1]{0:T(128)S(6)} %copy.11.mixing, f32[24,128]{1,0:T(8,128)} %get-tuple-element.9.memory, bf16[16,96,128]{2,1,0:T(8,128)(2,1)} %all_to_all.15.arrived, f32[2,64,128]{2,1,0:T(8,128)} %get-tuple-element.14.refs_0_), custom_call_target="tpu_custom_call" | custom-call | tf_op jit(solution)/shard_map/evolve/pallas_call | solution.py:249
  56.6 3.6 %all-to-all-start.2 = ((bf16[16,24,256]{2,1,0:T(8,128)(2,1)}), bf16[16,24,256]{2,1,0:T(8,128)(2,1)S(1)}, u32[]{:S(2)}, u32[]{:S(2)}) async-start(bf16[16,24,256]{2,1,0:T(8,128)(2,1)} %evolve.3), calls=%async_computation.2 | async-start | bytes 393216 | tf_op jit(solution)/shard_map/all_to_all | solution.py:280
  60.2 0.1 collective-permute-start.1
  60.3 1.6 %collective-permute-done.1.trace = bf16[16,24,256]{2,1,0:T(8,128)(2,1)S(1)} collective-permute-done((bf16[16,24,256]{2,1,0:T(8,128)(2,1)}, bf16[16,24,256]{2,1,0:T(8,128)(2,1)S(1)}, u32[]{:S(2)}, u32[]{:S(2)}) %collective-permute-start.1) | collective-permute-done | bytes 196640 | tf_op jit(solution)/shard_map/ppermute | solution.py:262
  61.9 0.0 copy-start.3
  61.9 0.7 copy-done.3
  62.6 3.3 %remap.1 = f32[24,4,1024]{2,1,0:T(4,128)} custom-call(bf16[16,24,256]{2,1,0:T(8,128)(2,1)} %copy-done.3, bf16[16,256,256]{2,1,0:T(8,128)(2,1)} %bitcast.9), custom_call_target="tpu_custom_call" | custom-call | tf_op jit(solution)/shard_map/remap/pallas_call | solution.py:272
  65.9 2.4 %all-to-all-done.2.history = bf16[16,24,256]{2,1,0:T(8,128)(2,1)S(1)} async-done(((bf16[16,24,256]{2,1,0:T(8,128)(2,1)}), bf16[16,24,256]{2,1,0:T(8,128)(2,1)S(1)}, u32[]{:S(2)}, u32[]{:S(2)}) %all-to-all-start.2) | async-done | bytes 196640 | tf_op jit(solution)/shard_map/all_to_all | solution.py:280
  68.3 0.0 copy-start.1
  68.3 0.7 copy-done.1
  69.0 3.6 %finish.1 = f32[20,4,1024]{2,1,0:T(4,128)} custom-call(bf16[16,24,256]{2,1,0:T(8,128)(2,1)} %copy-done.1, f32[20,4,1024]{2,1,0:T(4,128)} %bitcast.11, f32[2,24,128]{2,1,0:T(8,128)} %get-tuple-element.15.mats), custom_call_target="tpu_custom_call" | custom-call | tf_op jit(solution)/shard_map/finish/pallas_call | solution.py:281
Async XLA Ops:
  3.7 21.6 %all-to-all-start = ((bf16[16,104,128]{2,1,0:T(8,128)(2,1)}), bf16[16,104,128]{2,1,0:T(8,128)(2,1)S(1)}, u32[]{:S(2)}, u32[]{:S(2)}) async-start(bf16[16,104,128]{2,1,0:T(8,128)(2,1)} %get-tuple-element.10), calls=%async_computation | async-start | bytes 851968 | tf_op jit(solution)/shard_map/all_to_all | solution.py:245
  25.3 0.8 %copy-start = (bf16[16,104,128]{2,1,0:T(8,128)(2,1)}, bf16[16,104,128]{2,1,0:T(8,128)(2,1)S(1)}, u32[]{:S(2)}) copy-start(bf16[16,104,128]{2,1,0:T(8,128)(2,1)S(1)} %all-to-all-done.arrived) | copy-start | bytes 1277956
  29.8 1.7 %collective-permute-start = (bf16[16,24,256]{2,1,0:T(8,128)(2,1)}, bf16[16,24,256]{2,1,0:T(8,128)(2,1)S(1)}, u32[]{:S(2)}, u32[]{:S(2)}) collective-permute-start(bf16[16,24,256]{2,1,0:T(8,128)(2,1)} %get-tuple-element.11), channel_id=1, source_target_pairs={{0,16},{16,0},{1,17},{17,1},{2,18},{18,2},{3,19},{19,3},{4,20},{20... | collective-permute-start | bytes 589832 | tf_op jit(solution)/shard_map/ppermute | solution.py:262
  31.5 0.7 copy-start.2
  56.6 11.7 %all-to-all-start.2 = ((bf16[16,24,256]{2,1,0:T(8,128)(2,1)}), bf16[16,24,256]{2,1,0:T(8,128)(2,1)S(1)}, u32[]{:S(2)}, u32[]{:S(2)}) async-start(bf16[16,24,256]{2,1,0:T(8,128)(2,1)} %evolve.3), calls=%async_computation.2 | async-start | bytes 393216 | tf_op jit(solution)/shard_map/all_to_all | solution.py:280
  60.2 1.7 %collective-permute-start.1 = (bf16[16,24,256]{2,1,0:T(8,128)(2,1)}, bf16[16,24,256]{2,1,0:T(8,128)(2,1)S(1)}, u32[]{:S(2)}, u32[]{:S(2)}) collective-permute-start(bf16[16,24,256]{2,1,0:T(8,128)(2,1)} %evolve.3), channel_id=1, source_target_pairs={{0,16},{16,0},{1,17},{17,1},{2,18},{18,2},{3,19},{19,3},{4,20},{20... | collective-permute-start | bytes 589832 | tf_op jit(solution)/shard_map/ppermute | solution.py:262
  61.9 0.7 copy-start.3
  68.3 0.7 copy-start.1

commit v2 on v1

v2 whole, which is shorter than its diff:
```python
import functools
import math

import jax
import jax.numpy as jnp
from jax import lax
from jax.experimental import pallas as pl
from jax.experimental.pallas import tpu as pltpu
from jax.sharding import PartitionSpec as P

ITERS = 2
LANES = 128
SUBLANES = 8
SPARE = 4 << 20
EXACT = lax.Precision.HIGHEST
VMEM = pl.BlockSpec(memory_space=pltpu.VMEM)
HBM = pl.BlockSpec(memory_space=pltpu.HBM)


def size_of(leaf):
    rows = -(-leaf.shape[-2] // SUBLANES) * SUBLANES if len(leaf.shape) > 1 else SUBLANES
    lanes = -(-leaf.shape[-1] // LANES) * LANES
    return math.prod(leaf.shape[:-2]) * rows * lanes * 4


def run(kernel, out, arrays, scratch, far=0, outward=0, cost=1):
    leaves = jax.tree.leaves(out) + list(arrays[far:]) + [leaf for leaf in scratch if hasattr(leaf, "shape")]
    return pl.pallas_call(
        kernel,
        out_shape=out,
        in_specs=[HBM] * far + [VMEM] * (len(arrays) - far),
        out_specs=(VMEM,) * (len(out) - outward) + (HBM,) * outward if isinstance(out, tuple) else VMEM,
        scratch_shapes=[leaf if not isinstance(leaf, jax.ShapeDtypeStruct) else pltpu.VMEM(leaf.shape, leaf.dtype) for leaf in scratch],
        compiler_params=pltpu.CompilerParams(vmem_limit_bytes=sum(map(size_of, leaves)) + SPARE),
        cost_estimate=pl.CostEstimate(flops=cost * 1000000, bytes_accessed=0, transcendentals=0),
        name=getattr(kernel, "__name__", "evolve"),
    )(*[a if a.size == 1 else pltpu.with_memory_space_constraint(a, pltpu.HBM) for a in arrays[:far]], *arrays[far:])


def lane_of(shape):
    return lax.broadcasted_iota(jnp.int32, shape, len(shape) - 1)


def row_of(shape):
    return lax.broadcasted_iota(jnp.int32, shape, 0)


def tiles_of(width):
    return [pl.ds(k * LANES, LANES) for k in range(width // LANES)]


def windows(tile, count, face):
    half = (LANES - face) // 2
    for k in range(count):
        own, left, right = tile(k), tile((k - 1) % count), tile((k + 1) % count)
        lane = lane_of(own.shape)
        yield 2 * k, jnp.where(lane < face + half, own, left)
        yield 2 * k + 1, pltpu.roll(jnp.where(lane < half, right, own), face, axis=1)


def pick(lane, cuts, parts):
    out = parts[-1]
    for cut, part in zip(reversed(cuts), reversed(parts[:-1])):
        out = jnp.where(lane < cut, part, out)
    return out


def ship(drive, chunk, face):
    rows, steps, width = drive.shape
    lane = lane_of((SUBLANES, LANES))
    views = [windows(lambda k, p=p: drive[p, :, k * LANES : (k + 1) * LANES], width // LANES, face) for p in range(rows)]
    for group in zip(*views):
        early, middle, late = [[view[g * SUBLANES : (g + 1) * SUBLANES] for _, view in group] for g in range(3)]
        tiles = []
        for p in range(rows):
            near, far = pltpu.roll(late[p], 24, axis=1), pltpu.roll(late[p], LANES - 24, axis=1)
            tiles.append(pick(lane, (88, 96, 104), (early[p], near, far, early[p])))
        for p in range(0, rows, 2):
            near, far = pltpu.roll(middle[p + 1], 16, axis=1), pltpu.roll(middle[p + 1], LANES - 16, axis=1)
            tiles.append(pick(lane, (80, 96, 112), (middle[p], near, far, middle[p])))
        rest = middle[1::2] + late
        for first, second in zip(rest[::2], rest[1::2]):
            tiles.append(pick(lane, (face,), (first, pltpu.roll(second, face, axis=1))))
        for i, tile in enumerate(tiles):
            chunk[group[0][0], pl.ds(i * SUBLANES, SUBLANES), :] = tile.astype(jnp.bfloat16)


def landed(arrived, a, rows, face, g):
    lane = lane_of((SUBLANES, LANES))
    tile = lambda i: arrived[a, pl.ds(i * SUBLANES, SUBLANES), :].astype(jnp.float32)
    if g == 0:
        return [tile(p) for p in range(rows)]

    def rest(i):
        held = tile(rows + rows // 2 + i // 2)
        return pltpu.roll(held, face, axis=1) if i % 2 else held

    if g == 1:
        out = []
        for p in range(0, rows, 2):
            both = tile(rows + p // 2)
            near, far = pltpu.roll(both, LANES - 16, axis=1), pltpu.roll(both, 16, axis=1)
            out += [both, pick(lane, (face, 96), (rest(p // 2), near, far))]
        return out
    out = []
    for p in range(rows):
        both = tile(p)
        near, far = pltpu.roll(both, LANES - 24, axis=1), pltpu.roll(both, 24, axis=1)
        out.append(pick(lane, (face, 96), (rest(rows // 2 + p), near, far)))
    return out


def joined(first, second, face):
    out = []
    for j in range(first.shape[1] // LANES):
        cut = slice(j * LANES, (j + 1) * LANES)
        x, y = first[:, cut], second[:, cut]
        lane = lane_of(x.shape)
        out.append(jnp.where(lane < face, x, pltpu.roll(y, face, axis=1)))
        out.append(jnp.where(lane < face, pltpu.roll(x, face, axis=1), y))
    return out


def prepare(
    rates_far, vertical_far, mixing_far, regime_far, land_far, land_temp_far, state_far, guess_far, blocks_far,
    chunk, base, sea, mats, memory, blocks,
    xs, by_row, levels, drive, rates, vertical, mixing, regime, land, land_temp, state, guess, done,
):
    pairs = (
        (rates_far, rates),
        (vertical_far, vertical),
        (mixing_far, mixing),
        (regime_far, regime),
        (land_far, land),
        (land_temp_far, land_temp),
        (state_far, state),
        (guess_far, guess),
        (blocks_far, blocks),
    )
    copies = [pltpu.make_async_copy(far, near, done.at[i]) for i, (far, near) in enumerate(pairs)]
    for copy in copies:
        copy.start()
    for copy in copies[:3]:
        copy.wait()
    lev, rows, width = state.shape
    steps = guess.shape[0]
    padded = xs.shape[0] // (steps + 1)
    face = width // chunk.shape[0]

    shape = (padded, LANES)
    row, lane = row_of(shape), lane_of(shape)
    up = jnp.zeros(shape, jnp.float32)
    down = jnp.zeros(shape, jnp.float32)
    for l in range(lev - 1):
        up = jnp.where((row == l) & (row > 0), vertical[0, l], up)
        down = jnp.where(row == l + 1, vertical[0, l], down)
    keep = jnp.where(row == 0, 0.0, 1.0 - up - down)
    power = jnp.where((row == lane) & (row < lev), 1.0, 0.0)
    answer = jnp.zeros(shape, jnp.float32)
    for n in range(steps + 1):
        xs[pl.ds(n * padded, padded), :] = power
        if n == steps:
            break
        answer = jnp.where(lane == steps - 1 - n, power[:, 0:1], answer)
        power = keep * power + up * pltpu.roll(power, padded - 1, axis=0) + down * pltpu.roll(power, 1, axis=0)
    mats[0] = jnp.where(row == 0, 0.0, power)
    mats[1] = answer
    first = xs[pl.ds(1, steps, stride=padded), :]
    v0 = vertical[0, 0]
    memory[pl.ds(0, steps), :] = jnp.broadcast_to(v0 * first[:, 0:1], first.shape)
    shape = (SUBLANES, LANES)
    row = row_of(shape)
    known = jnp.where(row == 0, 1.0 - v0 - 4.0 * mixing[0, 0], mixing[0, 0])
    for kind in range(rates.shape[1]):
        known = jnp.where(row == 2 + kind, rates[0, kind], known)
    memory[pl.ds(steps, SUBLANES), :] = known
    for copy in copies[3:8]:
        copy.wait()
    to_below = jnp.where(lane_of(first.shape) == 0, 0.0, v0 * first)[:, :padded]

    coeff = jnp.zeros(regime.shape, jnp.float32)
    for kind in range(rates.shape[1]):
        coeff = jnp.where(regime[...] == kind, rates[0, kind], coeff)
    on_land = land[...] == 1
    sea[...] = jnp.where(on_land, 0.0, coeff)
    fixed = jnp.where(on_land, coeff * land_temp[...], 0.0)

    count = width // LANES
    rest = pl.ds(lev * rows, (padded - lev) * rows)
    for k, cut in enumerate(tiles_of(width)):
        for l in range(lev):
            levels[k, pl.ds(l * rows, rows), :] = state[l, :, cut]
        levels[k, rest, :] = jnp.zeros((rest.size, LANES), jnp.float32)
        for t in range(steps):
            by_row[k, pl.ds(t * rows, rows), :] = guess[t, :, cut]
    for p in range(rows):
        for k, cut in enumerate(tiles_of(width)):
            own = levels[k, pl.ds(p, padded, stride=rows), :]
            below = jnp.dot(to_below, own, precision=EXACT, preferred_element_type=jnp.float32)
            part = below + fixed[p : p + 1, k * LANES : (k + 1) * LANES]
            base[p, :, cut] = part
            drive[p, :, cut] = part + sea[p : p + 1, cut] * by_row[k, pl.ds(p, steps, stride=rows), :]
    ship(drive, chunk, face)
    fields = jnp.concatenate([state[0], regime[...].astype(jnp.float32)], axis=0)
    for a, window in windows(lambda k: fields[:, k * LANES : (k + 1) * LANES], count, face):
        chunk[a, pl.ds(chunk.shape[1] - 2 * rows, 2 * rows), :] = window.astype(jnp.bfloat16)
    copies[8].wait()


def evolve(first, last, memory, arrived, fields, trace, *refs):
    if last:
        away, drive, past, packed, done = refs
    else:
        drive, past, packed = refs
    tiles, steps, cells = trace.shape
    grid_rows = fields.shape[1]
    rows = grid_rows // tiles
    face = cells // rows
    groups = steps // SUBLANES
    side = pl.ds(SUBLANES, grid_rows)
    if first:
        for a in range(tiles):
            both = arrived[a, pl.ds(arrived.shape[1] - 2 * rows, 2 * rows), :].astype(jnp.float32)
            fields[0, pl.ds(a * rows, rows), :] = both[:rows]
            fields[1, pl.ds(a * rows, rows), :] = both[rows:]
        regime = fields[1]
        coeff = jnp.zeros(regime.shape, jnp.float32)
        for kind in range(memory.shape[0] - steps - 2):
            coeff = jnp.where(regime == kind, memory[steps + 2 + kind : steps + 3 + kind, :], coeff)
        fields[1] = memory[steps : steps + 1, :] - coeff
    mix = memory[steps + 1 : steps + 2, :]
    edge = jnp.zeros((SUBLANES, LANES), jnp.float32)
    for n in range(steps + 1):
        past[n, pl.ds(0, SUBLANES), :] = edge
        past[n, pl.ds(SUBLANES + grid_rows, SUBLANES), :] = edge
    lane = lane_of((tiles, LANES))

    def west(x, by=1):
        return pltpu.roll(x, by, axis=1)

    def east(x, by=1):
        return pltpu.roll(x, LANES - by, axis=1)

    def weight(j):
        return memory[j : j + 1, :]

    def receive(g):
        for a in range(tiles):
            for p, tile in enumerate(landed(arrived, a, rows, face, g)):
                drive[g, pl.ds((a * rows + p) * SUBLANES, SUBLANES), :] = tile

    def known(n, upto):
        total = drive[n // SUBLANES, pl.ds(n % SUBLANES, grid_rows, stride=SUBLANES), :]
        for k in range(upto):
            total = total + weight(n - k) * past[k, side, :]
        return total

    def beside(n):
        return past[n, pl.ds(SUBLANES - 1, grid_rows), :] + past[n, pl.ds(SUBLANES + 1, grid_rows), :]

    def keep(n, surface):
        past[n, side, :] = surface
        if n == 0:
            return
        g, t = (n - 1) // SUBLANES, (n - 1) % SUBLANES
        for j in range(cells // LANES):
            even = past[n, pl.ds(SUBLANES + 2 * j, tiles, stride=rows), :]
            odd = past[n, pl.ds(SUBLANES + 2 * j + 1, tiles, stride=rows), :]
            packed[j, g, pl.ds(t, tiles, stride=SUBLANES), :] = pick(lane, (face,), (even, pltpu.roll(odd, face, axis=1)))
        if t == SUBLANES - 1:
            now = pl.ds(g * SUBLANES, SUBLANES)
            for j in range(cells // LANES):
                for a in range(tiles):
                    tile = packed[j, g, pl.ds(a * SUBLANES, SUBLANES), :]
                    trace[a, now, pl.ds(j * LANES, LANES)] = tile.astype(jnp.bfloat16)
            if last:
                pltpu.make_async_copy(trace.at[:, now, :], away.at[:, now, :], done.at[g]).start()

    surface = fields[0]
    receive(0)
    keep(0, surface)
    stay = fields[1]
    stay_west, stay_east = west(stay), east(stay)
    before = None
    for n in range(0, steps, 2):
        if n % SUBLANES == 0 and n // SUBLANES + 1 < groups:
            receive(n // SUBLANES + 1)
        part = known(n, max(n - 1, 0))
        here, at_west, at_east = part, west(part), east(part)
        if before is not None:
            here = here + weight(1) * before[0]
            at_west = at_west + weight(1) * before[1]
            at_east = at_east + weight(1) * before[2]
        rim = beside(n)
        w1, e1, w2, e2 = west(surface), east(surface), west(surface, 2), east(surface, 2)
        next_here = (stay * surface + here) + mix * (rim + (w1 + e1))
        next_west = (stay_west * w1 + at_west) + mix * (west(rim) + (w2 + surface))
        next_east = (stay_east * e1 + at_east) + mix * (east(rim) + (surface + e2))
        keep(n + 1, next_here)
        surface = (stay * next_here + known(n + 1, n + 1)) + mix * (beside(n + 1) + (next_west + next_east))
        keep(n + 2, surface)
        before = (next_here, next_west, next_east)
    if last:
        for g in range(groups):
            now = pl.ds(g * SUBLANES, SUBLANES)
            pltpu.make_async_copy(trace.at[:, now, :], away.at[:, now, :], done.at[g]).wait()


def product(trace, regrid, a):
    return lax.dot_general(trace[a], regrid[a], (((1,), (1,)), ((), ())), preferred_element_type=jnp.float32)


def redrive(trace, regrid, base, sea, chunk, drive):
    tiles, steps, cells = trace.shape
    rows, _, width = base.shape
    face = cells // rows
    count = width // LANES
    for k, cut in enumerate(tiles_of(width)):
        mapped = joined(product(trace, regrid, 2 * k), product(trace, regrid, 2 * k + 1), face)
        for p in range(rows):
            drive[p, :, cut] = base[p, :, cut] + sea[p : p + 1, cut] * mapped[p]
    ship(drive, chunk, face)


def remap(trace, regrid, forcing, by_row):
    tiles, steps, cells = trace.shape
    _, rows, width = forcing.shape
    face = cells // rows
    for k, cut in enumerate(tiles_of(width)):
        mapped = joined(product(trace, regrid, 2 * k), product(trace, regrid, 2 * k + 1), face)
        for p in range(rows):
            by_row[k, pl.ds(p, steps, stride=rows), :] = mapped[p]
        for t in range(steps):
            forcing[t, :, cut] = by_row[k, pl.ds(t * rows, rows), :]


def unforced(state, mats, rest, stack, levels, by_row):
    lev, rows, width = state.shape
    padded = mats.shape[1]
    fill = pl.ds(lev * rows, (padded - lev) * rows)
    still = mats[0][:, :padded]
    for k, cut in enumerate(tiles_of(width)):
        for l in range(lev):
            levels[k, pl.ds(l * rows, rows), :] = state[l, :, cut]
        levels[k, fill, :] = jnp.zeros((fill.size, LANES), jnp.float32)
        for p in range(rows):
            own = levels[k, pl.ds(p, padded, stride=rows), :]
            end = jnp.dot(still, own, precision=EXACT, preferred_element_type=jnp.float32)
            by_row[k, pl.ds(p, padded, stride=rows), :] = end
        for l in range(lev):
            rest[l, :, cut] = by_row[k, pl.ds(l * rows, rows), :]
    left = mats[1]
    for i in range(stack.shape[0]):
        part = left.astype(jnp.bfloat16)
        stack[i] = part
        left = left - part.astype(jnp.float32)


def finish(history, rest, stack, final, by_row):
    tiles, steps, cells = history.shape
    lev, rows, width = rest.shape
    padded = stack.shape[1]
    face = cells // rows
    for k, cut in enumerate(tiles_of(width)):
        seen = joined(history[2 * k].astype(jnp.float32), history[2 * k + 1].astype(jnp.float32), face)
        for p in range(rows):
            end = None
            for i in range(stack.shape[0]):
                part = jnp.dot(
                    stack[i][:, :steps], seen[p].astype(jnp.bfloat16), preferred_element_type=jnp.float32
                )
                end = part if end is None else end + part
            by_row[k, pl.ds(p, padded, stride=rows), :] = end
        for l in range(lev):
            final[l, :, cut] = rest[l, :, cut] + by_row[k, pl.ds(l * rows, rows), :]


def on_device(state, guess, regrid, regime, land, land_temp, exchange_rate, vertical, mixing):
    _, lev, rows, width = state.shape
    steps = guess.shape[1]
    tiles = lax.axis_size("tile")
    face = width // tiles
    cells = rows * face
    grid_rows = rows * tiles
    if 2 * face != LANES or LANES - face < 2 * steps or 2 * rows != SUBLANES or steps != 3 * SUBLANES:
        raise ValueError("unsupported sizes")
    padded = -(-lev // SUBLANES) * SUBLANES
    f32, bf16 = jnp.float32, jnp.bfloat16
    shape = jax.ShapeDtypeStruct
    state, guess, blocks = state[0], guess[0], regrid[0, 0]

    count = width // LANES
    by_row = shape((count, steps * rows, LANES), f32)
    levels = shape((count, padded * rows, LANES), f32)
    fields_shape = shape((2, grid_rows, LANES), f32)
    trace_shape = shape((tiles, steps, cells), bf16)
    groups = steps // SUBLANES
    sent = rows * steps * 3 // 4
    drive = shape((rows, steps, width), f32)
    stepping = [
        shape((groups, grid_rows * SUBLANES, LANES), f32),
        shape((steps + 1, grid_rows + 2 * SUBLANES, LANES), f32),
        shape((cells // LANES, groups, tiles * SUBLANES, LANES), f32),
    ]

    arrays = (exchange_rate, vertical, mixing[None], regime[0], land[0], land_temp[0], state, guess, blocks)
    near = [pltpu.SMEM(a.shape, a.dtype) for a in arrays[:3]] + [shape(a.shape, a.dtype) for a in arrays[3:8]]
    chunk, base, sea, mats, memory, blocks = run(
        prepare,
        (
            shape((tiles, sent + 2 * rows, LANES), bf16),
            shape((rows, steps, width), f32),
            shape((rows, width), f32),
            shape((2, padded, LANES), f32),
            shape((steps + SUBLANES, LANES), f32),
            shape(blocks.shape, blocks.dtype),
        ),
        arrays,
        [shape(((steps + 1) * padded, LANES), f32), by_row, levels, drive] + near + [pltpu.SemaphoreType.DMA((len(arrays),))],
        far=len(arrays),
    )
    for sweep in range(ITERS):
        arrived = lax.all_to_all(chunk, "tile", split_axis=0, concat_axis=0, tiled=True)
        if sweep == 0:
            fields, trace = run(
                functools.partial(evolve, True, False), (fields_shape, trace_shape), (memory, arrived), stepping
            )
        else:
            trace, away = run(
                functools.partial(evolve, False, True),
                (trace_shape, trace_shape),
                (memory, arrived, fields),
                stepping + [pltpu.SemaphoreType.DMA((groups,))],
                outward=1,
            )
        partner = lax.ppermute(trace, "mp", [(0, 1), (1, 0)])
        if sweep < ITERS - 1:
            chunk = run(
                redrive,
                shape((tiles, sent, LANES), bf16),
                (partner, blocks, base, sea),
                [drive],
            )
    history = lax.all_to_all(away, "tile", split_axis=0, concat_axis=0, tiled=True)
    forcing = run(remap, shape((steps, rows, width), f32), (partner, blocks), [by_row])
    final_shape = shape((lev, rows, width), f32)
    rest, stack = run(unforced, (final_shape, shape((3, padded, LANES), bf16)), (state, mats), [levels, levels])
    final = run(finish, final_shape, (history, rest, stack), [levels])
    return final[None], forcing[None]


def solution(mesh):
    return jax.shard_map(
        on_device,
        mesh=mesh,
        in_specs=(
            P("mp", None, "tile", None),
            P("mp", None, "tile", None),
            P("mp", "tile", None, None, None),
            P("mp", "tile", None),
            P("mp", "tile", None),
            P("mp", "tile", None),
            P("mp", None),
            P("mp", None),
            P("mp"),
        ),
        out_specs=(P("mp", None, "tile", None), P("mp", None, "tile", None)),
        check_vma=False,
    )
```

time: 73.1 us -> 58.8 us (0.80)
  blocking collectives: 17.4 us -> 33.8 us
  waiting for transfers between devices: 18.3 us -> 6.87 us
  starting transfers between devices: 12 us -> 3.68 us
  Pallas kernels: 20.8 us -> 12.8 us
  local copies, waits for them, and re-layouts: 2.78 us -> 0.01 us
    all_to_all x1 -> x2, blocking collectives: 17.4 us -> 33.8 us  [on_device(): lax.all_to_all(chunk, 'tile', split_axis=0, concat_axis=0, tiled=True)]
    all_to_all x2 -> x1, waiting for transfers between devices: 15 us -> 4.94 us  [on_device(): lax.all_to_all(away, 'tile', split_axis=0, concat_axis=0, tiled=True)]
    all_to_all x2 -> x1, starting transfers between devices: 11.9 us -> 3.53 us  [on_device(): lax.all_to_all(away, 'tile', split_axis=0, concat_axis=0, tiled=True)]
    pallas_call x6 -> x7, Pallas kernels: 20.8 us -> 12.8 us  [run(): pl.pallas_call(kernel, out_shape=out, in_specs=[HBM] * far + [VMEM] * (le...]
    unnamed x8 -> x2, local copies, waits for them, and re-layouts: 2.78 us -> 0.01 us
    ppermute x2, waiting for transfers between devices: 3.29 us -> 1.92 us  [on_device(): partner = lax.ppermute(trace, 'mp', [(0, 1), (1, 0)])]
  transfers between devices with their start and end apart: 4 -> 3, of which waited for: 4 -> 3; matrix products, arithmetic and copies ran while one was open for 0% -> 0% of each run, Pallas kernels for 5% -> 4%
where the time goes in v2:
time: 58.8 us; the launch traced here: 58.5 us
  blocking collectives  33.8 us (57%)
  Pallas kernels  12.8 us (22%)
  waiting for transfers between devices  6.87 us (12%)
  starting transfers between devices  3.68 us (6%)
  between operations  1.35 us (2%)
    all_to_all x2, blocking collectives, on_device(): lax.all_to_all(chunk, 'tile', split_axis=0, concat_axis=0, tiled=True)  33.8 us
    pallas_call x7, Pallas kernels, run(): pl.pallas_call(kernel, out_shape=out, in_specs=[HBM] * far + [VMEM] * (le...  12.8 us
    all_to_all x1, waiting for transfers between devices, on_device(): lax.all_to_all(away, 'tile', split_axis=0, concat_axis=0, tiled=True)  4.94 us
    all_to_all x1, starting transfers between devices, on_device(): lax.all_to_all(away, 'tile', split_axis=0, concat_axis=0, tiled=True)  3.53 us
    ppermute x2, waiting for transfers between devices, on_device(): partner = lax.ppermute(trace, 'mp', [(0, 1), (1, 0)])  1.92 us
  transfers between devices with their start and end apart: 3, of which 3 were waited for; matrix products, arithmetic and copies ran while one was open for 0% of the time, Pallas kernels for 4%

profile of v2, /device:TPU:0, one launch (start us, length us, event | category | flops | bytes accessed | tf_op | source)
XLA Modules:
  0.0 58.5 jit_solution(17586977918639923640)
XLA Ops:
  1.3 2.8 %prepare.1 = (bf16[16,80,128]{2,1,0:T(8,128)(2,1)S(1)}, f32[4,24,1024]{2,1,0:T(8,128)S(1)}, f32[4,1024]{1,0:T(4,128)S(1)}, f32[2,24,128]{2,1,0:T(8,128)S(1)}, f3...) custom-call(f32[1,4]{1,0:T(1,128)} %rates_far.1, f32[1,19]{1,0:T(1,128)} %vertical_far.1, ...), custom_call_target="tpu_custom_call" | custom-call | flops 1000000 | tf_op jit(solution)/shard_map/prepare/pallas_call | solution.py:28
  4.0 19.5 %all_to_all.15.arrived = bf16[16,80,128]{2,1,0:T(8,128)(2,1)S(1)} all-to-all(bf16[16,80,128]{2,1,0:T(8,128)(2,1)S(1)} %get-tuple-element.15), channel_id=1, replica_groups=mesh['mp'=2,'tile'=16] {'tile'}, dimensions={0} | all-to-all | bytes 655360 | tf_op jit(solution)/shard_map/all_to_all | solution.py:423
  23.5 2.2 %evolve.2 = (f32[2,64,128]{2,1,0:T(8,128)S(1)}, bf16[16,24,256]{2,1,0:T(8,128)(2,1)S(1)}) custom-call(f32[32,128]{1,0:T(8,128)S(1)} %get-tuple-element.14.memory, bf16[16,80,128]{2,1,0:T(8,128)(2,1)S(1)} %all_to_all.15.arrived), custom_call_target="tpu_custom_call" | custom-call | flops 1000000 | tf_op jit(solution)/shard_map/evolve/pallas_call | solution.py:28
  25.8 0.1 collective-permute-start
  25.9 1.4 %collective-permute-done.trace = bf16[16,24,256]{2,1,0:T(8,128)(2,1)S(1)} collective-permute-done((bf16[16,24,256]{2,1,0:T(8,128)(2,1)S(1)}, bf16[16,24,256]{2,1,0:T(8,128)(2,1)S(1)}, u32[]{:S(2)}, u32[]{:S(2)}) %collective-permute-start) | collective-permute-done | bytes 196640 | tf_op jit(solution)/shard_map/ppermute | solution.py:436
  27.3 0.0 copy-start
  27.3 1.1 %redrive.1 = bf16[16,72,128]{2,1,0:T(8,128)(2,1)S(1)} custom-call(bf16[16,24,256]{2,1,0:T(8,128)(2,1)S(1)} %collective-permute-done.trace, bf16[16,256,256]{2,1,0:T(8,128)(2,1)S(1)} %get-tuple-element.17.regrid, f32[4,24,1024]{2,1,0:T(8,128)S(1)} %get-tuple-element.18.base, f32[4,1024]{1,0:T(4,128)S(1)} %get-tuple-element.19.sea), custom_call_target="tpu_custom_call" | custom-call | flops 1000000 | tf_op jit(solution)/shard_map/redrive/pallas_call | solution.py:28
  28.4 14.3 %all_to_all.16.arrived = bf16[16,72,128]{2,1,0:T(8,128)(2,1)S(1)} all-to-all(bf16[16,72,128]{2,1,0:T(8,128)(2,1)S(1)} %redrive.1), channel_id=1, replica_groups=mesh['mp'=2,'tile'=16] {'tile'}, dimensions={0} | all-to-all | bytes 589824 | tf_op jit(solution)/shard_map/all_to_all | solution.py:423
  42.7 2.9 %evolve.3 = (bf16[16,24,256]{2,1,0:T(8,128)(2,1)S(1)}, bf16[16,24,256]{2,1,0:T(8,128)(2,1)}) custom-call(f32[32,128]{1,0:T(8,128)S(1)} %get-tuple-element.14.memory, bf16[16,72,128]{2,1,0:T(8,128)(2,1)S(1)} %all_to_all.16.arrived, f32[2,64,128]{2,1,0:T(8,128)S(1)} %get-tuple-element.20.fields), custom_call_target="tpu_custom_call" | custom-call | flops 1000000 | tf_op jit(solution)/shard_map/evolve/pallas_call | solution.py:28
  45.6 3.5 %all-to-all-start.2 = ((bf16[16,24,256]{2,1,0:T(8,128)(2,1)}), bf16[16,24,256]{2,1,0:T(8,128)(2,1)S(1)}, u32[]{:S(2)}, u32[]{:S(2)}) async-start(bf16[16,24,256]{2,1,0:T(8,128)(2,1)} %get-tuple-element.21), calls=%async_computation.2 | async-start | bytes 393216 | tf_op jit(solution)/shard_map/all_to_all | solution.py:444
  49.2 0.1 collective-permute-start.1
  49.2 0.0 copy-done
  49.3 0.9 %unforced.1 = (f32[20,4,1024]{2,1,0:T(4,128)S(1)}, bf16[3,24,128]{2,1,0:T(8,128)(2,1)S(1)}) custom-call(f32[20,4,1024]{2,1,0:T(4,128)S(1)} %bitcast.11, f32[2,24,128]{2,1,0:T(8,128)S(1)} %get-tuple-element.22.mats), custom_call_target="tpu_custom_call" | custom-call | flops 1000000 | tf_op jit(solution)/shard_map/unforced/pallas_call | solution.py:28
  50.2 0.5 collective-permute-done.1.trace
  50.7 1.6 %remap.1 = f32[24,4,1024]{2,1,0:T(4,128)} custom-call(bf16[16,24,256]{2,1,0:T(8,128)(2,1)S(1)} %collective-permute-done.1.trace, bf16[16,256,256]{2,1,0:T(8,128)(2,1)S(1)} %get-tuple-element.17.regrid), custom_call_target="tpu_custom_call" | custom-call | flops 1000000 | tf_op jit(solution)/shard_map/remap/pallas_call | solution.py:28
  52.3 4.9 %all-to-all-done.2.history = bf16[16,24,256]{2,1,0:T(8,128)(2,1)S(1)} async-done(((bf16[16,24,256]{2,1,0:T(8,128)(2,1)}), bf16[16,24,256]{2,1,0:T(8,128)(2,1)S(1)}, u32[]{:S(2)}, u32[]{:S(2)}) %all-to-all-start.2) | async-done | bytes 196640 | tf_op jit(solution)/shard_map/all_to_all | solution.py:444
  57.2 1.3 %finish.1 = f32[20,4,1024]{2,1,0:T(4,128)} custom-call(bf16[16,24,256]{2,1,0:T(8,128)(2,1)S(1)} %all-to-all-done.2.history, f32[20,4,1024]{2,1,0:T(4,128)S(1)} %get-tuple-element.23.rest, bf16[3,24,128]{2,1,0:T(8,128)(2,1)S(1)} %get-tuple-element.24.stack), custom_call_target="tpu_custom_call" | custom-call | flops 1000000 | tf_op jit(solution)/shard_map/finish/pallas_call | solution.py:28
Async XLA Ops:
  25.8 1.5 %collective-permute-start = (bf16[16,24,256]{2,1,0:T(8,128)(2,1)S(1)}, bf16[16,24,256]{2,1,0:T(8,128)(2,1)S(1)}, u32[]{:S(2)}, u32[]{:S(2)}) collective-permute-start(bf16[16,24,256]{2,1,0:T(8,128)(2,1)S(1)} %get-tuple-element.16), channel_id=1, source_target_pairs={{0,16},{16,0},{1,17},{17,1},{2,18},{18,2},{3,19},{19,3},{4,20},{20... | collective-permute-start | bytes 589832 | tf_op jit(solution)/shard_map/ppermute | solution.py:436
  27.3 22.0 %copy-start = (f32[1,20,4,1024]{3,2,1,0:T(4,128)S(1)}, f32[1,20,4,1024]{3,2,1,0:T(4,128)}, u32[]{:S(2)}) copy-start(f32[1,20,4,1024]{3,2,1,0:T(4,128)} %param.9) | copy-start | bytes 983044
  45.6 11.6 %all-to-all-start.2 = ((bf16[16,24,256]{2,1,0:T(8,128)(2,1)}), bf16[16,24,256]{2,1,0:T(8,128)(2,1)S(1)}, u32[]{:S(2)}, u32[]{:S(2)}) async-start(bf16[16,24,256]{2,1,0:T(8,128)(2,1)} %get-tuple-element.21), calls=%async_computation.2 | async-start | bytes 393216 | tf_op jit(solution)/shard_map/all_to_all | solution.py:444
  49.2 1.5 %collective-permute-start.1 = (bf16[16,24,256]{2,1,0:T(8,128)(2,1)S(1)}, bf16[16,24,256]{2,1,0:T(8,128)(2,1)S(1)}, u32[]{:S(2)}, u32[]{:S(2)}) collective-permute-start(bf16[16,24,256]{2,1,0:T(8,128)(2,1)S(1)} %get-tuple-element.25), channel_id=1, source_target_pairs={{0,16},{16,0},{1,17},{17,1},{2,18},{18,2},{3,19},{19,3},{4,20},{20... | collective-permute-start | bytes 589832 | tf_op jit(solution)/shard_map/ppermute | solution.py:436

commit v3 on v2

--- a/solution.py
+++ b/solution.py
@@ -18,23 +18,25 @@
 
 
 def size_of(leaf):
-    rows = -(-leaf.shape[-2] // SUBLANES) * SUBLANES if len(leaf.shape) > 1 else SUBLANES
+    if len(leaf.shape) < 2:
+        return 4096
+    rows = -(-leaf.shape[-2] // SUBLANES) * SUBLANES
     lanes = -(-leaf.shape[-1] // LANES) * LANES
     return math.prod(leaf.shape[:-2]) * rows * lanes * 4
 
 
 def run(kernel, out, arrays, scratch, far=0, outward=0, cost=1):
-    leaves = jax.tree.leaves(out) + list(arrays[far:]) + [leaf for leaf in scratch if hasattr(leaf, "shape")]
+    leaves = jax.tree.leaves(out) + list(arrays[far:]) + [leaf for leaf in scratch if isinstance(leaf, jax.ShapeDtypeStruct)]
     return pl.pallas_call(
         kernel,
         out_shape=out,
         in_specs=[HBM] * far + [VMEM] * (len(arrays) - far),
-        out_specs=(VMEM,) * (len(out) - outward) + (HBM,) * outward if isinstance(out, tuple) else VMEM,
+        out_specs=(VMEM,) * (len(out) - outward) + (HBM,) * outward if isinstance(out, tuple) else (HBM if outward else VMEM),
         scratch_shapes=[leaf if not isinstance(leaf, jax.ShapeDtypeStruct) else pltpu.VMEM(leaf.shape, leaf.dtype) for leaf in scratch],
         compiler_params=pltpu.CompilerParams(vmem_limit_bytes=sum(map(size_of, leaves)) + SPARE),
         cost_estimate=pl.CostEstimate(flops=cost * 1000000, bytes_accessed=0, transcendentals=0),
         name=getattr(kernel, "__name__", "evolve"),
-    )(*[a if a.size == 1 else pltpu.with_memory_space_constraint(a, pltpu.HBM) for a in arrays[:far]], *arrays[far:])
+    )(*[pltpu.with_memory_space_constraint(a, pltpu.HBM) for a in arrays[:far]], *arrays[far:])
 
 
 def lane_of(shape):
@@ -122,29 +124,28 @@
 
 
 def prepare(
-    rates_far, vertical_far, mixing_far, regime_far, land_far, land_temp_far, state_far, guess_far, blocks_far,
-    chunk, base, sea, mats, memory, blocks,
-    xs, by_row, levels, drive, rates, vertical, mixing, regime, land, land_temp, state, guess, done,
+    rates_far, vertical_far, regime_far, land_far, land_temp_far, state_far, guess_far,
+    chunk, base, sea, memory, xs,
+    by_row, levels, drive, rates, vertical, regime, land, land_temp, state, guess, done,
 ):
     pairs = (
         (rates_far, rates),
         (vertical_far, vertical),
-        (mixing_far, mixing),
         (regime_far, regime),
         (land_far, land),
         (land_temp_far, land_temp),
         (state_far, state),
         (guess_far, guess),
-        (blocks_far, blocks),
     )
     copies = [pltpu.make_async_copy(far, near, done.at[i]) for i, (far, near) in enumerate(pairs)]
     for copy in copies:
         copy.start()
-    for copy in copies[:3]:
+    for copy in copies[:2]:
         copy.wait()
     lev, rows, width = state.shape
     steps = guess.shape[0]
-    padded = xs.shape[0] // (steps + 1)
+    padded = xs.shape[1]
+    deep = levels.shape[1] // rows
     face = width // chunk.shape[0]
 
     shape = (padded, LANES)
@@ -156,27 +157,29 @@
         down = jnp.where(row == l + 1, vertical[0, l], down)
     keep = jnp.where(row == 0, 0.0, 1.0 - up - down)
     power = jnp.where((row == lane) & (row < lev), 1.0, 0.0)
-    answer = jnp.zeros(shape, jnp.float32)
+    first = jnp.zeros((steps, LANES), jnp.float32)
     for n in range(steps + 1):
-        xs[pl.ds(n * padded, padded), :] = power
+        xs[n] = power
         if n == steps:
             break
-        answer = jnp.where(lane == steps - 1 - n, power[:, 0:1], answer)
+        first = jnp.where(row_of(first.shape) == n, power[1:2, :], first)
         power = keep * power + up * pltpu.roll(power, padded - 1, axis=0) + down * pltpu.roll(power, 1, axis=0)
-    mats[0] = jnp.where(row == 0, 0.0, power)
-    mats[1] = answer
-    first = xs[pl.ds(1, steps, stride=padded), :]
     v0 = vertical[0, 0]
     memory[pl.ds(0, steps), :] = jnp.broadcast_to(v0 * first[:, 0:1], first.shape)
     shape = (SUBLANES, LANES)
     row = row_of(shape)
-    known = jnp.where(row == 0, 1.0 - v0 - 4.0 * mixing[0, 0], mixing[0, 0])
+    known = jnp.full(shape, v0, jnp.float32)
     for kind in range(rates.shape[1]):
-        known = jnp.where(row == 2 + kind, rates[0, kind], known)
+        known = jnp.where(row == 1 + kind, rates[0, kind], known)
     memory[pl.ds(steps, SUBLANES), :] = known
-    for copy in copies[3:8]:
+    for copy in copies[2:]:
         copy.wait()
-    to_below = jnp.where(lane_of(first.shape) == 0, 0.0, v0 * first)[:, :padded]
+    to_below = jnp.where(lane_of(first.shape) == 0, 0.0, v0 * first)
+    high = to_below.astype(jnp.bfloat16).astype(jnp.float32)
+    low = to_below - high
+    lane = lane_of(first.shape)
+    to_below = pick(lane, (deep, 2 * deep), (high, pltpu.roll(high, deep, axis=1), pltpu.roll(low, 2 * deep, axis=1)))
+    to_below = to_below[:, : 3 * deep].astype(jnp.bfloat16)
 
     coeff = jnp.zeros(regime.shape, jnp.float32)
     for kind in range(rates.shape[1]):
@@ -186,7 +189,7 @@
     fixed = jnp.where(on_land, coeff * land_temp[...], 0.0)
 
     count = width // LANES
-    rest = pl.ds(lev * rows, (padded - lev) * rows)
+    rest = pl.ds(lev * rows, (deep - lev) * rows)
     for k, cut in enumerate(tiles_of(width)):
         for l in range(lev):
             levels[k, pl.ds(l * rows, rows), :] = state[l, :, cut]
@@ -194,24 +197,31 @@
         for t in range(steps):
             by_row[k, pl.ds(t * rows, rows), :] = guess[t, :, cut]
     for p in range(rows):
-        for k, cut in enumerate(tiles_of(width)):
-            own = levels[k, pl.ds(p, padded, stride=rows), :]
-            below = jnp.dot(to_below, own, precision=EXACT, preferred_element_type=jnp.float32)
-            part = below + fixed[p : p + 1, k * LANES : (k + 1) * LANES]
-            base[p, :, cut] = part
-            drive[p, :, cut] = part + sea[p : p + 1, cut] * by_row[k, pl.ds(p, steps, stride=rows), :]
+        for k in range(0, count, 2):
+            parts = []
+            for i in (k, k + 1):
+                own = levels[i, pl.ds(p, deep, stride=rows), :]
+                near = own.astype(jnp.bfloat16)
+                parts.append(jnp.concatenate([near, (own - near.astype(jnp.float32)).astype(jnp.bfloat16), near], axis=0))
+            pair = jnp.dot(to_below, jnp.concatenate(parts, axis=1), preferred_element_type=jnp.float32)
+            for i in (k, k + 1):
+                cut = pl.ds(i * LANES, LANES)
+                part = pair[:, (i - k) * LANES : (i - k + 1) * LANES] + fixed[p : p + 1, i * LANES : (i + 1) * LANES]
+                base[p, :, cut] = part
+                drive[p, :, cut] = part + sea[p : p + 1, cut] * by_row[i, pl.ds(p, steps, stride=rows), :]
     ship(drive, chunk, face)
     fields = jnp.concatenate([state[0], regime[...].astype(jnp.float32)], axis=0)
     for a, window in windows(lambda k: fields[:, k * LANES : (k + 1) * LANES], count, face):
         chunk[a, pl.ds(chunk.shape[1] - 2 * rows, 2 * rows), :] = window.astype(jnp.bfloat16)
-    copies[8].wait()
-
-
-def evolve(first, last, memory, arrived, fields, trace, *refs):
-    if last:
-        away, drive, past, packed, done = refs
+
+
+def evolve(first, last, *refs):
+    if first:
+        blocks_far, mixing, memory, arrived, fields, trace, blocks, drive, past, packed, fetched = refs
+        fetch = pltpu.make_async_copy(blocks_far, blocks, fetched)
+        fetch.start()
     else:
-        drive, past, packed = refs
+        memory, arrived, fields, trace, away, drive, past, packed, done = refs
     tiles, steps, cells = trace.shape
     grid_rows = fields.shape[1]
     rows = grid_rows // tiles
@@ -225,10 +235,12 @@
             fields[1, pl.ds(a * rows, rows), :] = both[rows:]
         regime = fields[1]
         coeff = jnp.zeros(regime.shape, jnp.float32)
-        for kind in range(memory.shape[0] - steps - 2):
-            coeff = jnp.where(regime == kind, memory[steps + 2 + kind : steps + 3 + kind, :], coeff)
-        fields[1] = memory[steps : steps + 1, :] - coeff
-    mix = memory[steps + 1 : steps + 2, :]
+        for kind in range(memory.shape[0] - steps - 1):
+            coeff = jnp.where(regime == kind, memory[steps + 1 + kind : steps + 2 + kind, :], coeff)
+        mix = jnp.broadcast_to(mixing[...].reshape(1, 1), coeff.shape)
+        fields[1] = 1.0 - memory[steps : steps + 1, :] - coeff - 4.0 * mix
+        fields[2] = mix
+    mix = fields[2, 0:1, :]
     edge = jnp.zeros((SUBLANES, LANES), jnp.float32)
     for n in range(steps + 1):
         past[n, pl.ds(0, SUBLANES), :] = edge
@@ -280,30 +292,22 @@
     receive(0)
     keep(0, surface)
     stay = fields[1]
-    stay_west, stay_east = west(stay), east(stay)
-    before = None
     for n in range(0, steps, 2):
         if n % SUBLANES == 0 and n // SUBLANES + 1 < groups:
             receive(n // SUBLANES + 1)
-        part = known(n, max(n - 1, 0))
-        here, at_west, at_east = part, west(part), east(part)
-        if before is not None:
-            here = here + weight(1) * before[0]
-            at_west = at_west + weight(1) * before[1]
-            at_east = at_east + weight(1) * before[2]
-        rim = beside(n)
-        w1, e1, w2, e2 = west(surface), east(surface), west(surface, 2), east(surface, 2)
-        next_here = (stay * surface + here) + mix * (rim + (w1 + e1))
-        next_west = (stay_west * w1 + at_west) + mix * (west(rim) + (w2 + surface))
-        next_east = (stay_east * e1 + at_east) + mix * (east(rim) + (surface + e2))
-        keep(n + 1, next_here)
-        surface = (stay * next_here + known(n + 1, n + 1)) + mix * (beside(n + 1) + (next_west + next_east))
+        still = (stay * surface + known(n, n)) + mix * beside(n)
+        middle = still + mix * (west(surface) + east(surface))
+        twice = (west(surface, 2) + east(surface, 2)) + (surface + surface)
+        sides = (west(still) + east(still)) + mix * twice
+        keep(n + 1, middle)
+        surface = (stay * middle + known(n + 1, n + 1)) + mix * (beside(n + 1) + sides)
         keep(n + 2, surface)
-        before = (next_here, next_west, next_east)
     if last:
         for g in range(groups):
             now = pl.ds(g * SUBLANES, SUBLANES)
             pltpu.make_async_copy(trace.at[:, now, :], away.at[:, now, :], done.at[g]).wait()
+    if first:
+        fetch.wait()
 
 
 def product(trace, regrid, a):
@@ -334,11 +338,13 @@
             forcing[t, :, cut] = by_row[k, pl.ds(t * rows, rows), :]
 
 
-def unforced(state, mats, rest, stack, levels, by_row):
+def unforced(state, powers, rest, stack, levels, by_row):
     lev, rows, width = state.shape
-    padded = mats.shape[1]
+    padded = powers.shape[1]
+    steps = powers.shape[0] - 1
     fill = pl.ds(lev * rows, (padded - lev) * rows)
-    still = mats[0][:, :padded]
+    row, lane = row_of(powers.shape[1:]), lane_of(powers.shape[1:])
+    still = jnp.where(row == 0, 0.0, powers[steps])[:, :padded]
     for k, cut in enumerate(tiles_of(width)):
         for l in range(lev):
             levels[k, pl.ds(l * rows, rows), :] = state[l, :, cut]
@@ -349,14 +355,16 @@
             by_row[k, pl.ds(p, padded, stride=rows), :] = end
         for l in range(lev):
             rest[l, :, cut] = by_row[k, pl.ds(l * rows, rows), :]
-    left = mats[1]
+    left = jnp.zeros(row.shape, jnp.float32)
+    for n in range(steps):
+        left = jnp.where(lane == steps - 1 - n, powers[n][:, 0:1], left)
     for i in range(stack.shape[0]):
         part = left.astype(jnp.bfloat16)
         stack[i] = part
         left = left - part.astype(jnp.float32)
 
 
-def finish(history, rest, stack, final, by_row):
+def finish(history, rest, stack, final_far, final, by_row, done):
     tiles, steps, cells = history.shape
     lev, rows, width = rest.shape
     padded = stack.shape[1]
@@ -372,7 +380,10 @@
                 end = part if end is None else end + part
             by_row[k, pl.ds(p, padded, stride=rows), :] = end
         for l in range(lev):
-            final[l, :, cut] = rest[l, :, cut] + by_row[k, pl.ds(l * rows, rows), :]
+            final[k, l] = rest[l, :, cut] + by_row[k, pl.ds(l * rows, rows), :]
+        pltpu.make_async_copy(final.at[k], final_far.at[:, :, cut], done.at[k]).start()
+    for k, cut in enumerate(tiles_of(width)):
+        pltpu.make_async_copy(final.at[k], final_far.at[:, :, cut], done.at[k]).wait()
 
 
 def on_device(state, guess, regrid, regime, land, land_temp, exchange_rate, vertical, mixing):
@@ -392,7 +403,7 @@
     count = width // LANES
     by_row = shape((count, steps * rows, LANES), f32)
     levels = shape((count, padded * rows, LANES), f32)
-    fields_shape = shape((2, grid_rows, LANES), f32)
+    fields_shape = shape((3, grid_rows, LANES), f32)
     trace_shape = shape((tiles, steps, cells), bf16)
     groups = steps // SUBLANES
     sent = rows * steps * 3 // 4
@@ -403,27 +414,30 @@
         shape((cells // LANES, groups, tiles * SUBLANES, LANES), f32),
     ]
 
-    arrays = (exchange_rate, vertical, mixing[None], regime[0], land[0], land_temp[0], state, guess, blocks)
-    near = [pltpu.SMEM(a.shape, a.dtype) for a in arrays[:3]] + [shape(a.shape, a.dtype) for a in arrays[3:8]]
-    chunk, base, sea, mats, memory, blocks = run(
+    arrays = (exchange_rate, vertical, regime[0], land[0], land_temp[0], state, guess)
+    near = [pltpu.SMEM(a.shape, a.dtype) for a in arrays[:2]] + [shape(a.shape, a.dtype) for a in arrays[2:]]
+    chunk, base, sea, memory, powers = run(
         prepare,
         (
             shape((tiles, sent + 2 * rows, LANES), bf16),
             shape((rows, steps, width), f32),
             shape((rows, width), f32),
-            shape((2, padded, LANES), f32),
             shape((steps + SUBLANES, LANES), f32),
-            shape(blocks.shape, blocks.dtype),
+            shape((steps + 1, padded, LANES), f32),
         ),
         arrays,
-        [shape(((steps + 1) * padded, LANES), f32), by_row, levels, drive] + near + [pltpu.SemaphoreType.DMA((len(arrays),))],
+        [by_row, shape((count, 4 * SUBLANES * rows, LANES), f32), drive] + near + [pltpu.SemaphoreType.DMA((len(arrays),))],
         far=len(arrays),
     )
     for sweep in range(ITERS):
         arrived = lax.all_to_all(chunk, "tile", split_axis=0, concat_axis=0, tiled=True)
         if sweep == 0:
-            fields, trace = run(
-                functools.partial(evolve, True, False), (fields_shape, trace_shape), (memory, arrived), stepping
+            fields, trace, blocks = run(
+                functools.partial(evolve, True, False),
+                (fields_shape, trace_shape, shape(blocks.shape, blocks.dtype)),
+                (blocks, mixing, memory, arrived),
+                stepping + [pltpu.SemaphoreType.DMA(())],
+                far=1,
             )
         else:
             trace, away = run(
@@ -444,8 +458,14 @@
     history = lax.all_to_all(away, "tile", split_axis=0, concat_axis=0, tiled=True)
     forcing = run(remap, shape((steps, rows, width), f32), (partner, blocks), [by_row])
     final_shape = shape((lev, rows, width), f32)
-    rest, stack = run(unforced, (final_shape, shape((3, padded, LANES), bf16)), (state, mats), [levels, levels])
-    final = run(finish, final_shape, (history, rest, stack), [levels])
+    rest, stack = run(unforced, (final_shape, shape((3, padded, LANES), bf16)), (state, powers), [levels, levels])
+    final = run(
+        finish,
+        final_shape,
+        (history, rest, stack),
+        [shape((count, lev, rows, LANES), f32), levels, pltpu.SemaphoreType.DMA((count,))],
+        outward=1,
+    )
     return final[None], forcing[None]
 
 

time: 58.8 us -> 57 us (0.969)
  blocking collectives: 33.8 us -> 14.3 us
  waiting for transfers between devices: 6.87 us -> 17.5 us
  starting transfers between devices: 3.68 us -> 12 us
  Pallas kernels: 12.8 us -> 11.5 us
    all_to_all x2 -> x1, blocking collectives: 33.8 us -> 14.3 us  [on_device(): lax.all_to_all(chunk, 'tile', split_axis=0, concat_axis=0, tiled=True)]
    all_to_all x0 -> x1, waiting for transfers between devices: none -> 10.7 us  [on_device(): lax.all_to_all(chunk, 'tile', split_axis=0, concat_axis=0, tiled=True)]
    all_to_all x0 -> x1, starting transfers between devices: none -> 8.35 us  [on_device(): lax.all_to_all(chunk, 'tile', split_axis=0, concat_axis=0, tiled=True)]
    pallas_call x7, Pallas kernels: 12.8 us -> 11.5 us  [run(): pl.pallas_call(kernel, out_shape=out, in_specs=[HBM] * far + [VMEM] * (le...]
  transfers between devices with their start and end apart: 3 -> 4, of which waited for: 3 -> 4; matrix products, arithmetic and copies ran while one was open for 0% -> 0% of each run, Pallas kernels for 4% -> 4%
where the time goes in v3:
time: 57 us; the launch traced here: 56.7 us
  waiting for transfers between devices  17.5 us (31%)
  blocking collectives  14.3 us (25%)
  starting transfers between devices  12 us (21%)
  Pallas kernels  11.5 us (20%)
  between operations  1.36 us (2%)
    all_to_all x1, blocking collectives, on_device(): lax.all_to_all(chunk, 'tile', split_axis=0, concat_axis=0, tiled=True)  14.3 us
    pallas_call x7, Pallas kernels, run(): pl.pallas_call(kernel, out_shape=out, in_specs=[HBM] * far + [VMEM] * (le...  11.5 us
    all_to_all x1, waiting for transfers between devices, on_device(): lax.all_to_all(chunk, 'tile', split_axis=0, concat_axis=0, tiled=True)  10.7 us
    all_to_all x1, starting transfers between devices, on_device(): lax.all_to_all(chunk, 'tile', split_axis=0, concat_axis=0, tiled=True)  8.35 us
    all_to_all x1, waiting for transfers between devices, on_device(): lax.all_to_all(away, 'tile', split_axis=0, concat_axis=0, tiled=True)  4.94 us
    all_to_all x1, starting transfers between devices, on_device(): lax.all_to_all(away, 'tile', split_axis=0, concat_axis=0, tiled=True)  3.53 us
    ppermute x2, waiting for transfers between devices, on_device(): partner = lax.ppermute(trace, 'mp', [(0, 1), (1, 0)])  1.93 us
  transfers between devices with their start and end apart: 4, of which 4 were waited for; matrix products, arithmetic and copies ran while one was open for 0% of the time, Pallas kernels for 4%

profile of v3, /device:TPU:0, one launch (start us, length us, event | category | flops | bytes accessed | tf_op | source)
XLA Modules:
  0.0 56.7 jit_solution(16986856487947867556)
XLA Ops:
  0.6 2.5 %prepare.1 = (bf16[16,80,128]{2,1,0:T(8,128)(2,1)}, f32[4,24,1024]{2,1,0:T(8,128)S(1)}, f32[4,1024]{1,0:T(4,128)S(1)}, f32[32,128]{1,0:T(8,128)S(1)}, f32[25,24,128]{2,1,0:T(8,128)S(1)}) custom-call(f32[1,4]{1,0:T(1,128)} %rates_far.1, f32[1,19]{1,0:T(1,128)} %vertical_far.1, s32[4,1024]{1,0:T(4,128)} %bitcast.14, s32[4,1024]{1,0:T(4,128)} %bitcast.15, ...), custom_call_target="tpu_custom_call" | custom-call | flops 1000000 | tf_op jit(solution)/shard_map/prepare/pallas_call | solution.py:30
  3.2 8.4 %all-to-all-start = ((bf16[16,80,128]{2,1,0:T(8,128)(2,1)}), bf16[16,80,128]{2,1,0:T(8,128)(2,1)S(1)}, u32[]{:S(2)}, u32[]{:S(2)}) async-start(bf16[16,80,128]{2,1,0:T(8,128)(2,1)} %get-tuple-element.15), calls=%async_computation | async-start | bytes 655360 | tf_op jit(solution)/shard_map/all_to_all | solution.py:433
  12.2 10.7 %all-to-all-done.refs_3_ = bf16[16,80,128]{2,1,0:T(8,128)(2,1)S(1)} async-done(((bf16[16,80,128]{2,1,0:T(8,128)(2,1)}), bf16[16,80,128]{2,1,0:T(8,128)(2,1)S(1)}, u32[]{:S(2)}, u32[]{:S(2)}) %all-to-all-start) | async-done | bytes 327712 | tf_op jit(solution)/shard_map/all_to_all | solution.py:433
  22.9 1.7 %evolve.2 = (f32[3,64,128]{2,1,0:T(8,128)S(1)}, bf16[16,24,256]{2,1,0:T(8,128)(2,1)S(1)}, bf16[16,256,256]{2,1,0:T(8,128)(2,1)S(1)}) custom-call(bf16[16,256,256]{2,1,0:T(8,128)(2,1)} %bitcast.10, f32[1]{0:T(128)S(6)} %copy.11.refs_1_, f32[32,128]{1,0:T(8,128)S(1)} %get-tuple-element.14.refs_2_.refs_0_, bf16[16,80,128]{2,1,0:T(8,128)(2,1)S(1)} %all-to-all-done.refs_3_), custom_call_target="tpu_custom_call" | custom-call | flops 1000000 | tf_op jit(solution)/shard_map/evolve/pallas_call | solution.py:30
  24.5 0.1 collective-permute-start
  24.6 1.4 %collective-permute-done.trace = bf16[16,24,256]{2,1,0:T(8,128)(2,1)S(1)} collective-permute-done((bf16[16,24,256]{2,1,0:T(8,128)(2,1)S(1)}, bf16[16,24,256]{2,1,0:T(8,128)(2,1)S(1)}, u32[]{:S(2)}, u32[]{:S(2)}) %collective-permute-start) | collective-permute-done | bytes 196640 | tf_op jit(solution)/shard_map/ppermute | solution.py:450
  26.0 0.0 copy-start
  26.0 1.1 %redrive.1 = bf16[16,72,128]{2,1,0:T(8,128)(2,1)S(1)} custom-call(bf16[16,24,256]{2,1,0:T(8,128)(2,1)S(1)} %collective-permute-done.trace, bf16[16,256,256]{2,1,0:T(8,128)(2,1)S(1)} %get-tuple-element.17.regrid, f32[4,24,1024]{2,1,0:T(8,128)S(1)} %get-tuple-element.18.base, f32[4,1024]{1,0:T(4,128)S(1)} %get-tuple-element.19.sea), custom_call_target="tpu_custom_call" | custom-call | flops 1000000 | tf_op jit(solution)/shard_map/redrive/pallas_call | solution.py:30
  27.2 14.3 %all_to_all.15.refs_1_ = bf16[16,72,128]{2,1,0:T(8,128)(2,1)S(1)} all-to-all(bf16[16,72,128]{2,1,0:T(8,128)(2,1)S(1)} %redrive.1), channel_id=1, replica_groups=mesh['mp'=2,'tile'=16] {'tile'}, dimensions={0} | all-to-all | bytes 589824 | tf_op jit(solution)/shard_map/all_to_all | solution.py:433
  41.5 2.4 %evolve.3 = (bf16[16,24,256]{2,1,0:T(8,128)(2,1)S(1)}, bf16[16,24,256]{2,1,0:T(8,128)(2,1)}) custom-call(f32[32,128]{1,0:T(8,128)S(1)} %get-tuple-element.14.refs_2_.refs_0_, bf16[16,72,128]{2,1,0:T(8,128)(2,1)S(1)} %all_to_all.15.refs_1_, f32[3,64,128]{2,1,0:T(8,128)S(1)} %get-tuple-element.20.refs_2_), custom_call_target="tpu_custom_call" | custom-call | flops 1000000 | tf_op jit(solution)/shard_map/evolve/pallas_call | solution.py:30
  43.9 3.5 %all-to-all-start.2 = ((bf16[16,24,256]{2,1,0:T(8,128)(2,1)}), bf16[16,24,256]{2,1,0:T(8,128)(2,1)S(1)}, u32[]{:S(2)}, u32[]{:S(2)}) async-start(bf16[16,24,256]{2,1,0:T(8,128)(2,1)} %get-tuple-element.21), calls=%async_computation.2 | async-start | bytes 393216 | tf_op jit(solution)/shard_map/all_to_all | solution.py:458
  47.4 0.1 collective-permute-start.1
  47.5 0.0 copy-done
  47.5 0.9 %unforced.1 = (f32[20,4,1024]{2,1,0:T(4,128)S(1)}, bf16[3,24,128]{2,1,0:T(8,128)(2,1)S(1)}) custom-call(f32[20,4,1024]{2,1,0:T(4,128)S(1)} %bitcast.9, f32[25,24,128]{2,1,0:T(8,128)S(1)} %get-tuple-element.22.powers), custom_call_target="tpu_custom_call" | custom-call | flops 1000000 | tf_op jit(solution)/shard_map/unforced/pallas_call | solution.py:30
  48.4 0.5 collective-permute-done.1.trace
  48.9 1.6 %remap.1 = f32[24,4,1024]{2,1,0:T(4,128)} custom-call(bf16[16,24,256]{2,1,0:T(8,128)(2,1)S(1)} %collective-permute-done.1.trace, bf16[16,256,256]{2,1,0:T(8,128)(2,1)S(1)} %get-tuple-element.17.regrid), custom_call_target="tpu_custom_call" | custom-call | flops 1000000 | tf_op jit(solution)/shard_map/remap/pallas_call | solution.py:30
  50.5 4.9 %all-to-all-done.2.history = bf16[16,24,256]{2,1,0:T(8,128)(2,1)S(1)} async-done(((bf16[16,24,256]{2,1,0:T(8,128)(2,1)}), bf16[16,24,256]{2,1,0:T(8,128)(2,1)S(1)}, u32[]{:S(2)}, u32[]{:S(2)}) %all-to-all-start.2) | async-done | bytes 196640 | tf_op jit(solution)/shard_map/all_to_all | solution.py:458
  55.4 1.2 %finish.1 = f32[20,4,1024]{2,1,0:T(4,128)} custom-call(bf16[16,24,256]{2,1,0:T(8,128)(2,1)S(1)} %all-to-all-done.2.history, f32[20,4,1024]{2,1,0:T(4,128)S(1)} %get-tuple-element.23.rest, bf16[3,24,128]{2,1,0:T(8,128)(2,1)S(1)} %get-tuple-element.24.stack), custom_call_target="tpu_custom_call" | custom-call | flops 1000000 | tf_op jit(solution)/shard_map/finish/pallas_call | solution.py:30
Async XLA Ops:
  3.2 19.7 %all-to-all-start = ((bf16[16,80,128]{2,1,0:T(8,128)(2,1)}), bf16[16,80,128]{2,1,0:T(8,128)(2,1)S(1)}, u32[]{:S(2)}, u32[]{:S(2)}) async-start(bf16[16,80,128]{2,1,0:T(8,128)(2,1)} %get-tuple-element.15), calls=%async_computation | async-start | bytes 655360 | tf_op jit(solution)/shard_map/all_to_all | solution.py:433
  24.5 1.5 %collective-permute-start = (bf16[16,24,256]{2,1,0:T(8,128)(2,1)S(1)}, bf16[16,24,256]{2,1,0:T(8,128)(2,1)S(1)}, u32[]{:S(2)}, u32[]{:S(2)}) collective-permute-start(bf16[16,24,256]{2,1,0:T(8,128)(2,1)S(1)} %get-tuple-element.16), channel_id=1, source_target_pairs={{0,16},{16,0},{1,17},{17,1},{2,18},{18,2},{3,19},{19,3},{4,20},{20... | collective-permute-start | bytes 589832 | tf_op jit(solution)/shard_map/ppermute | solution.py:450
  26.0 21.4 %copy-start = (f32[1,20,4,1024]{3,2,1,0:T(4,128)S(1)}, f32[1,20,4,1024]{3,2,1,0:T(4,128)}, u32[]{:S(2)}) copy-start(f32[1,20,4,1024]{3,2,1,0:T(4,128)} %param.9) | copy-start | bytes 983044
  43.9 11.6 %all-to-all-start.2 = ((bf16[16,24,256]{2,1,0:T(8,128)(2,1)}), bf16[16,24,256]{2,1,0:T(8,128)(2,1)S(1)}, u32[]{:S(2)}, u32[]{:S(2)}) async-start(bf16[16,24,256]{2,1,0:T(8,128)(2,1)} %get-tuple-element.21), calls=%async_computation.2 | async-start | bytes 393216 | tf_op jit(solution)/shard_map/all_to_all | solution.py:458
  47.4 1.5 %collective-permute-start.1 = (bf16[16,24,256]{2,1,0:T(8,128)(2,1)S(1)}, bf16[16,24,256]{2,1,0:T(8,128)(2,1)S(1)}, u32[]{:S(2)}, u32[]{:S(2)}) collective-permute-start(bf16[16,24,256]{2,1,0:T(8,128)(2,1)S(1)} %get-tuple-element.25), channel_id=1, source_target_pairs={{0,16},{16,0},{1,17},{17,1},{2,18},{18,2},{3,19},{19,3},{4,20},{20... | collective-permute-start | bytes 589832 | tf_op jit(solution)/shard_map/ppermute | solution.py:450

commit v4 on v3

--- a/solution.py
+++ b/solution.py
@@ -36,7 +36,7 @@
         compiler_params=pltpu.CompilerParams(vmem_limit_bytes=sum(map(size_of, leaves)) + SPARE),
         cost_estimate=pl.CostEstimate(flops=cost * 1000000, bytes_accessed=0, transcendentals=0),
         name=getattr(kernel, "__name__", "evolve"),
-    )(*[pltpu.with_memory_space_constraint(a, pltpu.HBM) for a in arrays[:far]], *arrays[far:])
+    )(*[a if a.size == 1 else pltpu.with_memory_space_constraint(a, pltpu.HBM) for a in arrays[:far]], *arrays[far:])
 
 
 def lane_of(shape):
@@ -60,6 +60,22 @@
         yield 2 * k + 1, pltpu.roll(jnp.where(lane < half, right, own), face, axis=1)
 
 
+def exchanged(x, y, face):
+    lane = lane_of(x.shape)
+    return (
+        jnp.where(lane < face, x, pltpu.roll(y, face, axis=1)),
+        jnp.where(lane < face, pltpu.roll(x, face, axis=1), y),
+    )
+
+
+def joined(first, second, face):
+    out = []
+    for j in range(first.shape[1] // LANES):
+        cut = slice(j * LANES, (j + 1) * LANES)
+        out += exchanged(first[:, cut], second[:, cut], face)
+    return out
+
+
 def pick(lane, cuts, parts):
     out = parts[-1]
     for cut, part in zip(reversed(cuts), reversed(parts[:-1])):
@@ -67,80 +83,65 @@
     return out
 
 
+def turn(x, by):
+    return pltpu.roll(x, by % LANES, axis=1)
+
+
 def ship(drive, chunk, face):
-    rows, steps, width = drive.shape
-    lane = lane_of((SUBLANES, LANES))
-    views = [windows(lambda k, p=p: drive[p, :, k * LANES : (k + 1) * LANES], width // LANES, face) for p in range(rows)]
-    for group in zip(*views):
-        early, middle, late = [[view[g * SUBLANES : (g + 1) * SUBLANES] for _, view in group] for g in range(3)]
-        tiles = []
-        for p in range(rows):
-            near, far = pltpu.roll(late[p], 24, axis=1), pltpu.roll(late[p], LANES - 24, axis=1)
-            tiles.append(pick(lane, (88, 96, 104), (early[p], near, far, early[p])))
-        for p in range(0, rows, 2):
-            near, far = pltpu.roll(middle[p + 1], 16, axis=1), pltpu.roll(middle[p + 1], LANES - 16, axis=1)
-            tiles.append(pick(lane, (80, 96, 112), (middle[p], near, far, middle[p])))
-        rest = middle[1::2] + late
-        for first, second in zip(rest[::2], rest[1::2]):
-            tiles.append(pick(lane, (face,), (first, pltpu.roll(second, face, axis=1))))
-        for i, tile in enumerate(tiles):
-            chunk[group[0][0], pl.ds(i * SUBLANES, SUBLANES), :] = tile.astype(jnp.bfloat16)
-
-
-def landed(arrived, a, rows, face, g):
+    tiles, pairs, _, _ = drive.shape
+    lane = lane_of((SUBLANES, LANES)) % face
+    for a in range(tiles):
+        own, halo = {}, {}
+        for j in range(pairs):
+            for g in range(3):
+                now = pl.ds(g * SUBLANES, SUBLANES)
+                own[j, g] = drive[a, j, now, :]
+                halo[j, g] = pick(lane, (face // 2,), (drive[(a + 1) % tiles, j, now, :], drive[(a - 1) % tiles, j, now, :]))
+        out = [own[j, g] for j in range(pairs) for g in range(3)]
+        for j in range(pairs):
+            out.append(pick(lane, (24, 32, 40), (halo[j, 0], turn(halo[j, 2], 24), turn(halo[j, 2], -24), halo[j, 0])))
+        out.append(pick(lane, (16, 32, 48), (halo[0, 1], turn(halo[1, 1], 16), turn(halo[1, 1], -16), halo[0, 1])))
+        for i, tile in enumerate(out):
+            chunk[a, pl.ds(i * SUBLANES, SUBLANES), :] = tile.astype(jnp.bfloat16)
+
+
+def landed(arrived, a, face, g):
     lane = lane_of((SUBLANES, LANES))
     tile = lambda i: arrived[a, pl.ds(i * SUBLANES, SUBLANES), :].astype(jnp.float32)
-    if g == 0:
-        return [tile(p) for p in range(rows)]
-
-    def rest(i):
-        held = tile(rows + rows // 2 + i // 2)
-        return pltpu.roll(held, face, axis=1) if i % 2 else held
-
-    if g == 1:
-        out = []
-        for p in range(0, rows, 2):
-            both = tile(rows + p // 2)
-            near, far = pltpu.roll(both, LANES - 16, axis=1), pltpu.roll(both, 16, axis=1)
-            out += [both, pick(lane, (face, 96), (rest(p // 2), near, far))]
-        return out
     out = []
-    for p in range(rows):
-        both = tile(p)
-        near, far = pltpu.roll(both, LANES - 24, axis=1), pltpu.roll(both, 24, axis=1)
-        out.append(pick(lane, (face, 96), (rest(rows // 2 + p), near, far)))
+    for j in range(2):
+        main = tile(3 * j + g)
+        halo = tile(8) if g == 1 else tile(6 + j)
+        if g == 0 or (g, j) == (1, 0):
+            out.append(pick(lane, (face,), (main, turn(halo, face))))
+            out.append(pick(lane, (face,), (turn(main, face), halo)))
+        else:
+            by = 16 if g == 1 else 24
+            out.append(pick(lane, (face, 96), (main, turn(halo, face - by), turn(halo, face + by))))
+            out.append(pick(lane, (face, 96), (turn(main, face), turn(halo, -by), turn(halo, by))))
     return out
 
 
-def joined(first, second, face):
-    out = []
-    for j in range(first.shape[1] // LANES):
-        cut = slice(j * LANES, (j + 1) * LANES)
-        x, y = first[:, cut], second[:, cut]
-        lane = lane_of(x.shape)
-        out.append(jnp.where(lane < face, x, pltpu.roll(y, face, axis=1)))
-        out.append(jnp.where(lane < face, pltpu.roll(x, face, axis=1), y))
-    return out
-
-
 def prepare(
-    rates_far, vertical_far, regime_far, land_far, land_temp_far, state_far, guess_far,
-    chunk, base, sea, memory, xs,
-    by_row, levels, drive, rates, vertical, regime, land, land_temp, state, guess, done,
+    rates_far, vertical_far, mixing_far, regime_far, land_far, land_temp_far, state_far, guess_far, blocks_far,
+    chunk, base, sea, memory, xs, blocks,
+    by_row, levels, drive, rates, vertical, mixing, regime, land, land_temp, state, guess, done,
 ):
     pairs = (
         (rates_far, rates),
         (vertical_far, vertical),
+        (mixing_far, mixing),
         (regime_far, regime),
         (land_far, land),
         (land_temp_far, land_temp),
         (state_far, state),
         (guess_far, guess),
+        (blocks_far.at[pl.ds(0, blocks.shape[0])], blocks),
     )
     copies = [pltpu.make_async_copy(far, near, done.at[i]) for i, (far, near) in enumerate(pairs)]
     for copy in copies:
         copy.start()
-    for copy in copies[:2]:
+    for copy in copies[:3]:
         copy.wait()
     lev, rows, width = state.shape
     steps = guess.shape[0]
@@ -168,13 +169,14 @@
     memory[pl.ds(0, steps), :] = jnp.broadcast_to(v0 * first[:, 0:1], first.shape)
     shape = (SUBLANES, LANES)
     row = row_of(shape)
-    known = jnp.full(shape, v0, jnp.float32)
+    known = jnp.where(row == 0, 1.0 - v0 - 4.0 * mixing[0, 0], mixing[0, 0])
     for kind in range(rates.shape[1]):
-        known = jnp.where(row == 1 + kind, rates[0, kind], known)
+        known = jnp.where(row == 2 + kind, rates[0, kind], known)
     memory[pl.ds(steps, SUBLANES), :] = known
-    for copy in copies[2:]:
+    for copy in copies[3:-1]:
         copy.wait()
-    to_below = jnp.where(lane_of(first.shape) == 0, 0.0, v0 * first)
+    own_cell = (lane_of(first.shape) == 0) & (row_of(first.shape) == 0)
+    to_below = jnp.where(own_cell, 1.0 - v0 - 4.0 * mixing[0, 0], v0 * first)
     high = to_below.astype(jnp.bfloat16).astype(jnp.float32)
     low = to_below - high
     lane = lane_of(first.shape)
@@ -185,40 +187,58 @@
     for kind in range(rates.shape[1]):
         coeff = jnp.where(regime[...] == kind, rates[0, kind], coeff)
     on_land = land[...] == 1
-    sea[...] = jnp.where(on_land, 0.0, coeff)
+    open_sea = jnp.where(on_land, 0.0, coeff)
     fixed = jnp.where(on_land, coeff * land_temp[...], 0.0)
+    left = state[0] - state[0].astype(jnp.bfloat16).astype(jnp.float32)
+    taken = coeff * left
 
     count = width // LANES
     rest = pl.ds(lev * rows, (deep - lev) * rows)
     for k, cut in enumerate(tiles_of(width)):
-        for l in range(lev):
+        levels[k, pl.ds(0, rows), :] = left[:, k * LANES : (k + 1) * LANES]
+        for l in range(1, lev):
             levels[k, pl.ds(l * rows, rows), :] = state[l, :, cut]
         levels[k, rest, :] = jnp.zeros((rest.size, LANES), jnp.float32)
         for t in range(steps):
             by_row[k, pl.ds(t * rows, rows), :] = guess[t, :, cut]
-    for p in range(rows):
+    def below(p, k):
+        parts = []
+        for i in (k, k + 1):
+            own = levels[i, pl.ds(p, deep, stride=rows), :]
+            near = own.astype(jnp.bfloat16)
+            parts.append(jnp.concatenate([near, (own - near.astype(jnp.float32)).astype(jnp.bfloat16), near], axis=0))
+        pair = jnp.dot(to_below, jnp.concatenate(parts, axis=1), preferred_element_type=jnp.float32)
+        return pair[:, :LANES], pair[:, LANES:]
+
+    for j in range(rows // 2):
+        two = (2 * j, 2 * j + 1)
         for k in range(0, count, 2):
-            parts = []
-            for i in (k, k + 1):
-                own = levels[i, pl.ds(p, deep, stride=rows), :]
-                near = own.astype(jnp.bfloat16)
-                parts.append(jnp.concatenate([near, (own - near.astype(jnp.float32)).astype(jnp.bfloat16), near], axis=0))
-            pair = jnp.dot(to_below, jnp.concatenate(parts, axis=1), preferred_element_type=jnp.float32)
-            for i in (k, k + 1):
-                cut = pl.ds(i * LANES, LANES)
-                part = pair[:, (i - k) * LANES : (i - k + 1) * LANES] + fixed[p : p + 1, i * LANES : (i + 1) * LANES]
-                base[p, :, cut] = part
-                drive[p, :, cut] = part + sea[p : p + 1, cut] * by_row[i, pl.ds(p, steps, stride=rows), :]
+            for i, *parts in zip((k, k + 1), *[below(p, k) for p in two]):
+                cut = slice(i * LANES, (i + 1) * LANES)
+                start = row_of(parts[0].shape) == 0
+                still = [part + jnp.where(start, fixed[p : p + 1, cut] - taken[p : p + 1, cut], fixed[p : p + 1, cut]) for p, part in zip(two, parts)]
+                slopes = [open_sea[p : p + 1, cut] for p in two]
+                forced = [
+                    part + slope * by_row[i, pl.ds(p, steps, stride=rows), :] for p, part, slope in zip(two, still, slopes)
+                ]
+                for b, tile in enumerate(exchanged(*still, face)):
+                    base[2 * i + b, j] = tile
+                for b, tile in enumerate(exchanged(*forced, face)):
+                    drive[2 * i + b, j] = tile
+                for b, tile in enumerate(exchanged(*slopes, face)):
+                    sea[pl.ds((2 * i + b) * (rows // 2) + j, 1), :] = tile
     ship(drive, chunk, face)
     fields = jnp.concatenate([state[0], regime[...].astype(jnp.float32)], axis=0)
     for a, window in windows(lambda k: fields[:, k * LANES : (k + 1) * LANES], count, face):
         chunk[a, pl.ds(chunk.shape[1] - 2 * rows, 2 * rows), :] = window.astype(jnp.bfloat16)
+    copies[-1].wait()
 
 
 def evolve(first, last, *refs):
     if first:
-        blocks_far, mixing, memory, arrived, fields, trace, blocks, drive, past, packed, fetched = refs
-        fetch = pltpu.make_async_copy(blocks_far, blocks, fetched)
+        blocks_far, memory, arrived, fields, trace, blocks, drive, past, packed, fetched = refs
+        half = blocks.shape[0]
+        fetch = pltpu.make_async_copy(blocks_far.at[pl.ds(half, half)], blocks, fetched)
         fetch.start()
     else:
         memory, arrived, fields, trace, away, drive, past, packed, done = refs
@@ -235,12 +255,10 @@
             fields[1, pl.ds(a * rows, rows), :] = both[rows:]
         regime = fields[1]
         coeff = jnp.zeros(regime.shape, jnp.float32)
-        for kind in range(memory.shape[0] - steps - 1):
-            coeff = jnp.where(regime == kind, memory[steps + 1 + kind : steps + 2 + kind, :], coeff)
-        mix = jnp.broadcast_to(mixing[...].reshape(1, 1), coeff.shape)
-        fields[1] = 1.0 - memory[steps : steps + 1, :] - coeff - 4.0 * mix
-        fields[2] = mix
-    mix = fields[2, 0:1, :]
+        for kind in range(memory.shape[0] - steps - 2):
+            coeff = jnp.where(regime == kind, memory[steps + 2 + kind : steps + 3 + kind, :], coeff)
+        fields[1] = memory[steps : steps + 1, :] - coeff
+    mix = memory[steps + 1 : steps + 2, :]
     edge = jnp.zeros((SUBLANES, LANES), jnp.float32)
     for n in range(steps + 1):
         past[n, pl.ds(0, SUBLANES), :] = edge
@@ -258,7 +276,7 @@
 
     def receive(g):
         for a in range(tiles):
-            for p, tile in enumerate(landed(arrived, a, rows, face, g)):
+            for p, tile in enumerate(landed(arrived, a, face, g)):
                 drive[g, pl.ds((a * rows + p) * SUBLANES, SUBLANES), :] = tile
 
     def known(n, upto):
@@ -310,23 +328,23 @@
         fetch.wait()
 
 
-def product(trace, regrid, a):
-    return lax.dot_general(trace[a], regrid[a], (((1,), (1,)), ((), ())), preferred_element_type=jnp.float32)
-
-
-def redrive(trace, regrid, base, sea, chunk, drive):
-    tiles, steps, cells = trace.shape
-    rows, _, width = base.shape
-    face = cells // rows
-    count = width // LANES
-    for k, cut in enumerate(tiles_of(width)):
-        mapped = joined(product(trace, regrid, 2 * k), product(trace, regrid, 2 * k + 1), face)
-        for p in range(rows):
-            drive[p, :, cut] = base[p, :, cut] + sea[p : p + 1, cut] * mapped[p]
-    ship(drive, chunk, face)
-
-
-def remap(trace, regrid, forcing, by_row):
+def product(trace, halves, a):
+    regrid, i = halves[a // halves[0].shape[0]], a % halves[0].shape[0]
+    return lax.dot_general(trace[a], regrid[i], (((1,), (1,)), ((), ())), preferred_element_type=jnp.float32)
+
+
+def redrive(trace, lower, upper, base, sea, chunk, drive):
+    tiles, pairs, _, _ = base.shape
+    for a in range(tiles):
+        mapped = product(trace, (lower, upper), a)
+        for j in range(pairs):
+            slope = sea[a * pairs + j : a * pairs + j + 1, :]
+            drive[a, j] = base[a, j] + slope * mapped[:, j * LANES : (j + 1) * LANES]
+    ship(drive, chunk, LANES // 2)
+
+
+def remap(trace, lower, upper, forcing, by_row):
+    regrid = (lower, upper)
     tiles, steps, cells = trace.shape
     _, rows, width = forcing.shape
     face = cells // rows
@@ -403,27 +421,29 @@
     count = width // LANES
     by_row = shape((count, steps * rows, LANES), f32)
     levels = shape((count, padded * rows, LANES), f32)
-    fields_shape = shape((3, grid_rows, LANES), f32)
+    fields_shape = shape((2, grid_rows, LANES), f32)
     trace_shape = shape((tiles, steps, cells), bf16)
     groups = steps // SUBLANES
     sent = rows * steps * 3 // 4
-    drive = shape((rows, steps, width), f32)
+    drive = shape((tiles, rows // 2, steps, LANES), f32)
     stepping = [
         shape((groups, grid_rows * SUBLANES, LANES), f32),
         shape((steps + 1, grid_rows + 2 * SUBLANES, LANES), f32),
         shape((cells // LANES, groups, tiles * SUBLANES, LANES), f32),
     ]
 
-    arrays = (exchange_rate, vertical, regime[0], land[0], land_temp[0], state, guess)
-    near = [pltpu.SMEM(a.shape, a.dtype) for a in arrays[:2]] + [shape(a.shape, a.dtype) for a in arrays[2:]]
-    chunk, base, sea, memory, powers = run(
+    arrays = (exchange_rate, vertical, mixing[None], regime[0], land[0], land_temp[0], state, guess, blocks)
+    half = shape((tiles // 2,) + blocks.shape[1:], blocks.dtype)
+    near = [pltpu.SMEM(a.shape, a.dtype) for a in arrays[:3]] + [shape(a.shape, a.dtype) for a in arrays[3:-1]]
+    chunk, base, sea, memory, powers, lower = run(
         prepare,
         (
             shape((tiles, sent + 2 * rows, LANES), bf16),
-            shape((rows, steps, width), f32),
-            shape((rows, width), f32),
+            drive,
+            shape((tiles * rows // 2, LANES), f32),
             shape((steps + SUBLANES, LANES), f32),
             shape((steps + 1, padded, LANES), f32),
+            half,
         ),
         arrays,
         [by_row, shape((count, 4 * SUBLANES * rows, LANES), f32), drive] + near + [pltpu.SemaphoreType.DMA((len(arrays),))],
@@ -432,10 +452,10 @@
     for sweep in range(ITERS):
         arrived = lax.all_to_all(chunk, "tile", split_axis=0, concat_axis=0, tiled=True)
         if sweep == 0:
-            fields, trace, blocks = run(
+            fields, trace, upper = run(
                 functools.partial(evolve, True, False),
-                (fields_shape, trace_shape, shape(blocks.shape, blocks.dtype)),
-                (blocks, mixing, memory, arrived),
+                (fields_shape, trace_shape, half),
+                (blocks, memory, arrived),
                 stepping + [pltpu.SemaphoreType.DMA(())],
                 far=1,
             )
@@ -452,11 +472,11 @@
             chunk = run(
                 redrive,
                 shape((tiles, sent, LANES), bf16),
-                (partner, blocks, base, sea),
+                (partner, lower, upper, base, sea),
                 [drive],
             )
     history = lax.all_to_all(away, "tile", split_axis=0, concat_axis=0, tiled=True)
-    forcing = run(remap, shape((steps, rows, width), f32), (partner, blocks), [by_row])
+    forcing = run(remap, shape((steps, rows, width), f32), (partner, lower, upper), [by_row])
     final_shape = shape((lev, rows, width), f32)
     rest, stack = run(unforced, (final_shape, shape((3, padded, LANES), bf16)), (state, powers), [levels, levels])
     final = run(

time: 57 us -> 56.8 us (level)
  blocking collectives: 14.3 us -> 33.7 us
  waiting for transfers between devices: 17.5 us -> 6.87 us
  starting transfers between devices: 12 us -> 3.68 us
  Pallas kernels: 11.5 us -> 10.8 us
    all_to_all x1 -> x2, blocking collectives: 14.3 us -> 33.7 us  [on_device(): lax.all_to_all(chunk, 'tile', split_axis=0, concat_axis=0, tiled=True)]
    all_to_all x1 -> x0, waiting for transfers between devices: 10.7 us -> none  [on_device(): lax.all_to_all(chunk, 'tile', split_axis=0, concat_axis=0, tiled=True)]
    all_to_all x1 -> x0, starting transfers between devices: 8.35 us -> none  [on_device(): lax.all_to_all(chunk, 'tile', split_axis=0, concat_axis=0, tiled=True)]
    pallas_call x7, Pallas kernels: 11.5 us -> 10.8 us  [run(): pl.pallas_call(kernel, out_shape=out, in_specs=[HBM] * far + [VMEM] * (le...]
  transfers between devices with their start and end apart: 4 -> 3, of which waited for: 4 -> 3; matrix products, arithmetic and copies ran while one was open for 0% -> 0% of each run, Pallas kernels for 4% -> 4%
where the time goes in v4:
time: 56.8 us; the launch traced here: 56.4 us
  blocking collectives  33.7 us (59%)
  Pallas kernels  10.8 us (19%)
  waiting for transfers between devices  6.87 us (12%)
  starting transfers between devices  3.68 us (6%)
  between operations  1.35 us (2%)
    all_to_all x2, blocking collectives, on_device(): lax.all_to_all(chunk, 'tile', split_axis=0, concat_axis=0, tiled=True)  33.7 us
    pallas_call x7, Pallas kernels, run(): pl.pallas_call(kernel, out_shape=out, in_specs=[HBM] * far + [VMEM] * (le...  10.8 us
    all_to_all x1, waiting for transfers between devices, on_device(): lax.all_to_all(away, 'tile', split_axis=0, concat_axis=0, tiled=True)  4.94 us
    all_to_all x1, starting transfers between devices, on_device(): lax.all_to_all(away, 'tile', split_axis=0, concat_axis=0, tiled=True)  3.53 us
    ppermute x2, waiting for transfers between devices, on_device(): partner = lax.ppermute(trace, 'mp', [(0, 1), (1, 0)])  1.93 us
  transfers between devices with their start and end apart: 3, of which 3 were waited for; matrix products, arithmetic and copies ran while one was open for 0% of the time, Pallas kernels for 4%

profile of v4, /device:TPU:0, one launch (start us, length us, event | category | flops | bytes accessed | tf_op | source)
XLA Modules:
  0.0 56.4 jit_solution(11965890018838845039)
XLA Ops:
  1.3 2.0 %prepare.1 = (bf16[16,80,128]{2,1,0:T(8,128)(2,1)S(1)}, f32[16,2,24,128]{3,2,1,0:T(8,128)S(1)}, f32[32,128]{1,0:T(8,128)S(1)}, f32[32,128]{1,0:T(8,128)S(1)}, f3...) custom-call(f32[1,4]{1,0:T(1,128)} %rates_far.1, f32[1,19]{1,0:T(1,128)} %vertical_far.1, ...), custom_call_target="tpu_custom_call" | custom-call | flops 1000000 | tf_op jit(solution)/shard_map/prepare/pallas_call | solution.py:30
  3.3 19.5 %all_to_all.15.refs_2_ = bf16[16,80,128]{2,1,0:T(8,128)(2,1)S(1)} all-to-all(bf16[16,80,128]{2,1,0:T(8,128)(2,1)S(1)} %get-tuple-element.16), channel_id=1, replica_groups=mesh['mp'=2,'tile'=16] {'tile'}, dimensions={0} | all-to-all | bytes 655360 | tf_op jit(solution)/shard_map/all_to_all | solution.py:453
  22.7 1.9 %evolve.2 = (f32[2,64,128]{2,1,0:T(8,128)S(1)}, bf16[16,24,256]{2,1,0:T(8,128)(2,1)S(1)}, bf16[8,256,256]{2,1,0:T(8,128)(2,1)S(1)}) custom-call(bf16[16,256,256]{2,1,0:T(8,128)(2,1)} %bitcast.13, f32[32,128]{1,0:T(8,128)S(1)} %get-tuple-element.15.refs_1_.refs_0_, bf16[16,80,128]{2,1,0:T(8,128)(2,1)S(1)} %all_to_all.15.refs_2_), custom_call_target="tpu_custom_call" | custom-call | flops 1000000 | tf_op jit(solution)/shard_map/evolve/pallas_call | solution.py:30
  24.6 0.1 collective-permute-start
  24.7 1.4 %collective-permute-done.trace = bf16[16,24,256]{2,1,0:T(8,128)(2,1)S(1)} collective-permute-done((bf16[16,24,256]{2,1,0:T(8,128)(2,1)S(1)}, bf16[16,24,256]{2,1,0:T(8,128)(2,1)S(1)}, u32[]{:S(2)}, u32[]{:S(2)}) %collective-permute-start) | collective-permute-done | bytes 196640 | tf_op jit(solution)/shard_map/ppermute | solution.py:470
  26.1 0.0 copy-start
  26.1 0.8 %redrive.1 = bf16[16,72,128]{2,1,0:T(8,128)(2,1)S(1)} custom-call(bf16[16,24,256]{2,1,0:T(8,128)(2,1)S(1)} %collective-permute-done.trace, bf16[8,256,256]{2,1,0:T(8,128)(2,1)S(1)} %get-tuple-element.18.lower, bf16[8,256,256]{2,1,0:T(8,128)(2,1)S(1)} %get-tuple-element.19.upper, f32[16,2,24,128]{3,2,1,0:T(8,128)S(1)} %get-tuple-element.20.base, ...), custom_call_target="tpu_custom_call" | custom-call | flops 1000000 | tf_op jit(solution)/shard_map/redrive/pallas_call | solution.py:30
  26.9 14.3 %all_to_all.16.refs_1_ = bf16[16,72,128]{2,1,0:T(8,128)(2,1)S(1)} all-to-all(bf16[16,72,128]{2,1,0:T(8,128)(2,1)S(1)} %redrive.1), channel_id=1, replica_groups=mesh['mp'=2,'tile'=16] {'tile'}, dimensions={0} | all-to-all | bytes 589824 | tf_op jit(solution)/shard_map/all_to_all | solution.py:453
  41.2 2.5 %evolve.3 = (bf16[16,24,256]{2,1,0:T(8,128)(2,1)S(1)}, bf16[16,24,256]{2,1,0:T(8,128)(2,1)}) custom-call(f32[32,128]{1,0:T(8,128)S(1)} %get-tuple-element.15.refs_1_.refs_0_, bf16[16,72,128]{2,1,0:T(8,128)(2,1)S(1)} %all_to_all.16.refs_1_, f32[2,64,128]{2,1,0:T(8,128)S(1)} %get-tuple-element.22.refs_2_), custom_call_target="tpu_custom_call" | custom-call | flops 1000000 | tf_op jit(solution)/shard_map/evolve/pallas_call | solution.py:30
  43.6 3.5 %all-to-all-start.2 = ((bf16[16,24,256]{2,1,0:T(8,128)(2,1)}), bf16[16,24,256]{2,1,0:T(8,128)(2,1)S(1)}, u32[]{:S(2)}, u32[]{:S(2)}) async-start(bf16[16,24,256]{2,1,0:T(8,128)(2,1)} %get-tuple-element.23), calls=%async_computation.2 | async-start | bytes 393216 | tf_op jit(solution)/shard_map/all_to_all | solution.py:478
  47.2 0.1 collective-permute-start.1
  47.3 0.0 copy-done
  47.3 0.9 %unforced.1 = (f32[20,4,1024]{2,1,0:T(4,128)S(1)}, bf16[3,24,128]{2,1,0:T(8,128)(2,1)S(1)}) custom-call(f32[20,4,1024]{2,1,0:T(4,128)S(1)} %bitcast.11, f32[25,24,128]{2,1,0:T(8,128)S(1)} %get-tuple-element.24.powers), custom_call_target="tpu_custom_call" | custom-call | flops 1000000 | tf_op jit(solution)/shard_map/unforced/pallas_call | solution.py:30
  48.2 0.5 collective-permute-done.1.trace
  48.7 1.6 %remap.1 = f32[24,4,1024]{2,1,0:T(4,128)} custom-call(bf16[16,24,256]{2,1,0:T(8,128)(2,1)S(1)} %collective-permute-done.1.trace, bf16[8,256,256]{2,1,0:T(8,128)(2,1)S(1)} %get-tuple-element.18.lower, bf16[8,256,256]{2,1,0:T(8,128)(2,1)S(1)} %get-tuple-element.19.upper), custom_call_target="tpu_custom_call" | custom-call | flops 1000000 | tf_op jit(solution)/shard_map/remap/pallas_call | solution.py:30
  50.3 4.9 %all-to-all-done.2.history = bf16[16,24,256]{2,1,0:T(8,128)(2,1)S(1)} async-done(((bf16[16,24,256]{2,1,0:T(8,128)(2,1)}), bf16[16,24,256]{2,1,0:T(8,128)(2,1)S(1)}, u32[]{:S(2)}, u32[]{:S(2)}) %all-to-all-start.2) | async-done | bytes 196640 | tf_op jit(solution)/shard_map/all_to_all | solution.py:478
  55.2 1.2 %finish.1 = f32[20,4,1024]{2,1,0:T(4,128)} custom-call(bf16[16,24,256]{2,1,0:T(8,128)(2,1)S(1)} %all-to-all-done.2.history, f32[20,4,1024]{2,1,0:T(4,128)S(1)} %get-tuple-element.25.rest, bf16[3,24,128]{2,1,0:T(8,128)(2,1)S(1)} %get-tuple-element.26.stack), custom_call_target="tpu_custom_call" | custom-call | flops 1000000 | tf_op jit(solution)/shard_map/finish/pallas_call | solution.py:30
Async XLA Ops:
  24.6 1.5 %collective-permute-start = (bf16[16,24,256]{2,1,0:T(8,128)(2,1)S(1)}, bf16[16,24,256]{2,1,0:T(8,128)(2,1)S(1)}, u32[]{:S(2)}, u32[]{:S(2)}) collective-permute-start(bf16[16,24,256]{2,1,0:T(8,128)(2,1)S(1)} %get-tuple-element.17), channel_id=1, source_target_pairs={{0,16},{16,0},{1,17},{17,1},{2,18},{18,2},{3,19},{19,3},{4,20},{20... | collective-permute-start | bytes 589832 | tf_op jit(solution)/shard_map/ppermute | solution.py:470
  26.1 21.2 %copy-start = (f32[1,20,4,1024]{3,2,1,0:T(4,128)S(1)}, f32[1,20,4,1024]{3,2,1,0:T(4,128)}, u32[]{:S(2)}) copy-start(f32[1,20,4,1024]{3,2,1,0:T(4,128)} %param.9) | copy-start | bytes 983044
  43.6 11.6 %all-to-all-start.2 = ((bf16[16,24,256]{2,1,0:T(8,128)(2,1)}), bf16[16,24,256]{2,1,0:T(8,128)(2,1)S(1)}, u32[]{:S(2)}, u32[]{:S(2)}) async-start(bf16[16,24,256]{2,1,0:T(8,128)(2,1)} %get-tuple-element.23), calls=%async_computation.2 | async-start | bytes 393216 | tf_op jit(solution)/shard_map/all_to_all | solution.py:478
  47.2 1.5 %collective-permute-start.1 = (bf16[16,24,256]{2,1,0:T(8,128)(2,1)S(1)}, bf16[16,24,256]{2,1,0:T(8,128)(2,1)S(1)}, u32[]{:S(2)}, u32[]{:S(2)}) collective-permute-start(bf16[16,24,256]{2,1,0:T(8,128)(2,1)S(1)} %get-tuple-element.27), channel_id=1, source_target_pairs={{0,16},{16,0},{1,17},{17,1},{2,18},{18,2},{3,19},{19,3},{4,20},{20... | collective-permute-start | bytes 589832 | tf_op jit(solution)/shard_map/ppermute | solution.py:470

commit v5 on v4

--- a/solution.py
+++ b/solution.py
@@ -248,6 +248,14 @@
     face = cells // rows
     groups = steps // SUBLANES
     side = pl.ds(SUBLANES, grid_rows)
+    edge = jnp.zeros((SUBLANES, LANES), jnp.float32)
+
+    @pl.loop(0, 5)
+    def _(part):
+        for n in range((steps + 1) // 5):
+            past[part * ((steps + 1) // 5) + n, pl.ds(0, SUBLANES), :] = edge
+            past[part * ((steps + 1) // 5) + n, pl.ds(SUBLANES + grid_rows, SUBLANES), :] = edge
+
     if first:
         for a in range(tiles):
             both = arrived[a, pl.ds(arrived.shape[1] - 2 * rows, 2 * rows), :].astype(jnp.float32)
@@ -259,10 +267,6 @@
             coeff = jnp.where(regime == kind, memory[steps + 2 + kind : steps + 3 + kind, :], coeff)
         fields[1] = memory[steps : steps + 1, :] - coeff
     mix = memory[steps + 1 : steps + 2, :]
-    edge = jnp.zeros((SUBLANES, LANES), jnp.float32)
-    for n in range(steps + 1):
-        past[n, pl.ds(0, SUBLANES), :] = edge
-        past[n, pl.ds(SUBLANES + grid_rows, SUBLANES), :] = edge
     lane = lane_of((tiles, LANES))
 
     def west(x, by=1):

time: 56.8 us -> 56.7 us (level)
  no operation moved by 1% of the time
where the time goes in v5:
time: 56.7 us; the launch traced here: 56.4 us
  blocking collectives  33.7 us (59%)
  Pallas kernels  10.7 us (19%)
  waiting for transfers between devices  6.87 us (12%)
  starting transfers between devices  3.68 us (6%)
  between operations  1.35 us (2%)
    all_to_all x2, blocking collectives, on_device(): lax.all_to_all(chunk, 'tile', split_axis=0, concat_axis=0, tiled=True)  33.7 us
    pallas_call x7, Pallas kernels, run(): pl.pallas_call(kernel, out_shape=out, in_specs=[HBM] * far + [VMEM] * (le...  10.7 us
    all_to_all x1, waiting for transfers between devices, on_device(): lax.all_to_all(away, 'tile', split_axis=0, concat_axis=0, tiled=True)  4.94 us
    all_to_all x1, starting transfers between devices, on_device(): lax.all_to_all(away, 'tile', split_axis=0, concat_axis=0, tiled=True)  3.53 us
    ppermute x2, waiting for transfers between devices, on_device(): partner = lax.ppermute(trace, 'mp', [(0, 1), (1, 0)])  1.93 us
  transfers between devices with their start and end apart: 3, of which 3 were waited for; matrix products, arithmetic and copies ran while one was open for 0% of the time, Pallas kernels for 4%

profile of v5, /device:TPU:0, one launch (start us, length us, event | category | flops | bytes accessed | tf_op | source)
XLA Modules:
  0.0 56.4 jit_solution(3846857887204456450)
XLA Ops:
  1.3 2.0 %prepare.1 = (bf16[16,80,128]{2,1,0:T(8,128)(2,1)S(1)}, f32[16,2,24,128]{3,2,1,0:T(8,128)S(1)}, f32[32,128]{1,0:T(8,128)S(1)}, f32[32,128]{1,0:T(8,128)S(1)}, f3...) custom-call(f32[1,4]{1,0:T(1,128)} %rates_far.1, f32[1,19]{1,0:T(1,128)} %vertical_far.1, ...), custom_call_target="tpu_custom_call" | custom-call | flops 1000000 | tf_op jit(solution)/shard_map/prepare/pallas_call | solution.py:30
  3.3 19.5 %all_to_all.15.refs_2_ = bf16[16,80,128]{2,1,0:T(8,128)(2,1)S(1)} all-to-all(bf16[16,80,128]{2,1,0:T(8,128)(2,1)S(1)} %get-tuple-element.16), channel_id=1, replica_groups=mesh['mp'=2,'tile'=16] {'tile'}, dimensions={0} | all-to-all | bytes 655360 | tf_op jit(solution)/shard_map/all_to_all | solution.py:457
  22.7 1.8 %evolve.2 = (f32[2,64,128]{2,1,0:T(8,128)S(1)}, bf16[16,24,256]{2,1,0:T(8,128)(2,1)S(1)}, bf16[8,256,256]{2,1,0:T(8,128)(2,1)S(1)}) custom-call(bf16[16,256,256]{2,1,0:T(8,128)(2,1)} %bitcast.13, f32[32,128]{1,0:T(8,128)S(1)} %get-tuple-element.15.refs_1_.refs_0_, bf16[16,80,128]{2,1,0:T(8,128)(2,1)S(1)} %all_to_all.15.refs_2_), custom_call_target="tpu_custom_call" | custom-call | flops 1000000 | tf_op jit(solution)/shard_map/evolve/pallas_call | solution.py:30
  24.5 0.1 collective-permute-start
  24.6 1.4 %collective-permute-done.trace = bf16[16,24,256]{2,1,0:T(8,128)(2,1)S(1)} collective-permute-done((bf16[16,24,256]{2,1,0:T(8,128)(2,1)S(1)}, bf16[16,24,256]{2,1,0:T(8,128)(2,1)S(1)}, u32[]{:S(2)}, u32[]{:S(2)}) %collective-permute-start) | collective-permute-done | bytes 196640 | tf_op jit(solution)/shard_map/ppermute | solution.py:474
  26.0 0.0 copy-start
  26.0 0.8 %redrive.1 = bf16[16,72,128]{2,1,0:T(8,128)(2,1)S(1)} custom-call(bf16[16,24,256]{2,1,0:T(8,128)(2,1)S(1)} %collective-permute-done.trace, bf16[8,256,256]{2,1,0:T(8,128)(2,1)S(1)} %get-tuple-element.18.lower, bf16[8,256,256]{2,1,0:T(8,128)(2,1)S(1)} %get-tuple-element.19.upper, f32[16,2,24,128]{3,2,1,0:T(8,128)S(1)} %get-tuple-element.20.base, ...), custom_call_target="tpu_custom_call" | custom-call | flops 1000000 | tf_op jit(solution)/shard_map/redrive/pallas_call | solution.py:30
  26.8 14.3 %all_to_all.16.refs_1_ = bf16[16,72,128]{2,1,0:T(8,128)(2,1)S(1)} all-to-all(bf16[16,72,128]{2,1,0:T(8,128)(2,1)S(1)} %redrive.1), channel_id=1, replica_groups=mesh['mp'=2,'tile'=16] {'tile'}, dimensions={0} | all-to-all | bytes 589824 | tf_op jit(solution)/shard_map/all_to_all | solution.py:457
  41.1 2.5 %evolve.3 = (bf16[16,24,256]{2,1,0:T(8,128)(2,1)S(1)}, bf16[16,24,256]{2,1,0:T(8,128)(2,1)}) custom-call(f32[32,128]{1,0:T(8,128)S(1)} %get-tuple-element.15.refs_1_.refs_0_, bf16[16,72,128]{2,1,0:T(8,128)(2,1)S(1)} %all_to_all.16.refs_1_, f32[2,64,128]{2,1,0:T(8,128)S(1)} %get-tuple-element.22.refs_2_), custom_call_target="tpu_custom_call" | custom-call | flops 1000000 | tf_op jit(solution)/shard_map/evolve/pallas_call | solution.py:30
  43.6 3.5 %all-to-all-start.2 = ((bf16[16,24,256]{2,1,0:T(8,128)(2,1)}), bf16[16,24,256]{2,1,0:T(8,128)(2,1)S(1)}, u32[]{:S(2)}, u32[]{:S(2)}) async-start(bf16[16,24,256]{2,1,0:T(8,128)(2,1)} %get-tuple-element.23), calls=%async_computation.2 | async-start | bytes 393216 | tf_op jit(solution)/shard_map/all_to_all | solution.py:482
  47.1 0.1 collective-permute-start.1
  47.2 0.0 copy-done
  47.2 0.9 %unforced.1 = (f32[20,4,1024]{2,1,0:T(4,128)S(1)}, bf16[3,24,128]{2,1,0:T(8,128)(2,1)S(1)}) custom-call(f32[20,4,1024]{2,1,0:T(4,128)S(1)} %bitcast.11, f32[25,24,128]{2,1,0:T(8,128)S(1)} %get-tuple-element.24.powers), custom_call_target="tpu_custom_call" | custom-call | flops 1000000 | tf_op jit(solution)/shard_map/unforced/pallas_call | solution.py:30
  48.1 0.5 collective-permute-done.1.trace
  48.6 1.6 %remap.1 = f32[24,4,1024]{2,1,0:T(4,128)} custom-call(bf16[16,24,256]{2,1,0:T(8,128)(2,1)S(1)} %collective-permute-done.1.trace, bf16[8,256,256]{2,1,0:T(8,128)(2,1)S(1)} %get-tuple-element.18.lower, bf16[8,256,256]{2,1,0:T(8,128)(2,1)S(1)} %get-tuple-element.19.upper), custom_call_target="tpu_custom_call" | custom-call | flops 1000000 | tf_op jit(solution)/shard_map/remap/pallas_call | solution.py:30
  50.2 4.9 %all-to-all-done.2.history = bf16[16,24,256]{2,1,0:T(8,128)(2,1)S(1)} async-done(((bf16[16,24,256]{2,1,0:T(8,128)(2,1)}), bf16[16,24,256]{2,1,0:T(8,128)(2,1)S(1)}, u32[]{:S(2)}, u32[]{:S(2)}) %all-to-all-start.2) | async-done | bytes 196640 | tf_op jit(solution)/shard_map/all_to_all | solution.py:482
  55.1 1.2 %finish.1 = f32[20,4,1024]{2,1,0:T(4,128)} custom-call(bf16[16,24,256]{2,1,0:T(8,128)(2,1)S(1)} %all-to-all-done.2.history, f32[20,4,1024]{2,1,0:T(4,128)S(1)} %get-tuple-element.25.rest, bf16[3,24,128]{2,1,0:T(8,128)(2,1)S(1)} %get-tuple-element.26.stack), custom_call_target="tpu_custom_call" | custom-call | flops 1000000 | tf_op jit(solution)/shard_map/finish/pallas_call | solution.py:30
Async XLA Ops:
  24.5 1.5 %collective-permute-start = (bf16[16,24,256]{2,1,0:T(8,128)(2,1)S(1)}, bf16[16,24,256]{2,1,0:T(8,128)(2,1)S(1)}, u32[]{:S(2)}, u32[]{:S(2)}) collective-permute-start(bf16[16,24,256]{2,1,0:T(8,128)(2,1)S(1)} %get-tuple-element.17), channel_id=1, source_target_pairs={{0,16},{16,0},{1,17},{17,1},{2,18},{18,2},{3,19},{19,3},{4,20},{20... | collective-permute-start | bytes 589832 | tf_op jit(solution)/shard_map/ppermute | solution.py:474
  26.0 21.2 %copy-start = (f32[1,20,4,1024]{3,2,1,0:T(4,128)S(1)}, f32[1,20,4,1024]{3,2,1,0:T(4,128)}, u32[]{:S(2)}) copy-start(f32[1,20,4,1024]{3,2,1,0:T(4,128)} %param.9) | copy-start | bytes 983044
  43.6 11.6 %all-to-all-start.2 = ((bf16[16,24,256]{2,1,0:T(8,128)(2,1)}), bf16[16,24,256]{2,1,0:T(8,128)(2,1)S(1)}, u32[]{:S(2)}, u32[]{:S(2)}) async-start(bf16[16,24,256]{2,1,0:T(8,128)(2,1)} %get-tuple-element.23), calls=%async_computation.2 | async-start | bytes 393216 | tf_op jit(solution)/shard_map/all_to_all | solution.py:482
  47.1 1.5 %collective-permute-start.1 = (bf16[16,24,256]{2,1,0:T(8,128)(2,1)S(1)}, bf16[16,24,256]{2,1,0:T(8,128)(2,1)S(1)}, u32[]{:S(2)}, u32[]{:S(2)}) collective-permute-start(bf16[16,24,256]{2,1,0:T(8,128)(2,1)S(1)} %get-tuple-element.27), channel_id=1, source_target_pairs={{0,16},{16,0},{1,17},{17,1},{2,18},{18,2},{3,19},{19,3},{4,20},{20... | collective-permute-start | bytes 589832 | tf_op jit(solution)/shard_map/ppermute | solution.py:474

commit v6 on v5

--- a/solution.py
+++ b/solution.py
@@ -380,30 +380,33 @@
     left = jnp.zeros(row.shape, jnp.float32)
     for n in range(steps):
         left = jnp.where(lane == steps - 1 - n, powers[n][:, 0:1], left)
-    for i in range(stack.shape[0]):
+    for i in range(stack.shape[0] // padded):
         part = left.astype(jnp.bfloat16)
-        stack[i] = part
+        stack[pl.ds(i * padded, padded), :] = part
         left = left - part.astype(jnp.float32)
 
 
 def finish(history, rest, stack, final_far, final, by_row, done):
     tiles, steps, cells = history.shape
     lev, rows, width = rest.shape
-    padded = stack.shape[1]
+    padded = by_row.shape[1] // rows
     face = cells // rows
-    for k, cut in enumerate(tiles_of(width)):
-        seen = joined(history[2 * k].astype(jnp.float32), history[2 * k + 1].astype(jnp.float32), face)
+    parts = stack[:, :steps]
+    cuts = tiles_of(width)
+    for k in range(0, len(cuts), 2):
+        near = [
+            joined(history[2 * i].astype(jnp.float32), history[2 * i + 1].astype(jnp.float32), face) for i in (k, k + 1)
+        ]
         for p in range(rows):
-            end = None
-            for i in range(stack.shape[0]):
-                part = jnp.dot(
-                    stack[i][:, :steps], seen[p].astype(jnp.bfloat16), preferred_element_type=jnp.float32
-                )
-                end = part if end is None else end + part
-            by_row[k, pl.ds(p, padded, stride=rows), :] = end
-        for l in range(lev):
-            final[k, l] = rest[l, :, cut] + by_row[k, pl.ds(l * rows, rows), :]
-        pltpu.make_async_copy(final.at[k], final_far.at[:, :, cut], done.at[k]).start()
+            seen = jnp.concatenate([near[0][p], near[1][p]], axis=1).astype(jnp.bfloat16)
+            ends = jnp.dot(parts, seen, preferred_element_type=jnp.float32)
+            end = (ends[:padded] + ends[padded : 2 * padded]) + ends[2 * padded :]
+            by_row[k, pl.ds(p, padded, stride=rows), :] = end[:, :LANES]
+            by_row[k + 1, pl.ds(p, padded, stride=rows), :] = end[:, LANES:]
+        for i in (k, k + 1):
+            for l in range(lev):
+                final[i, l] = rest[l, :, cuts[i]] + by_row[i, pl.ds(l * rows, rows), :]
+            pltpu.make_async_copy(final.at[i], final_far.at[:, :, cuts[i]], done.at[i]).start()
     for k, cut in enumerate(tiles_of(width)):
         pltpu.make_async_copy(final.at[k], final_far.at[:, :, cut], done.at[k]).wait()
 
@@ -482,7 +485,7 @@
     history = lax.all_to_all(away, "tile", split_axis=0, concat_axis=0, tiled=True)
     forcing = run(remap, shape((steps, rows, width), f32), (partner, lower, upper), [by_row])
     final_shape = shape((lev, rows, width), f32)
-    rest, stack = run(unforced, (final_shape, shape((3, padded, LANES), bf16)), (state, powers), [levels, levels])
+    rest, stack = run(unforced, (final_shape, shape((3 * padded, LANES), bf16)), (state, powers), [levels, levels])
     final = run(
         finish,
         final_shape,

time: 56.7 us -> 56.6 us (level)
  no operation moved by 1% of the time
where the time goes in v6:
time: 56.6 us; the launch traced here: 56.2 us
  blocking collectives  33.7 us (60%)
  Pallas kernels  10.6 us (19%)
  waiting for transfers between devices  6.87 us (12%)
  starting transfers between devices  3.68 us (7%)
  between operations  1.35 us (2%)
    all_to_all x2, blocking collectives, on_device(): lax.all_to_all(chunk, 'tile', split_axis=0, concat_axis=0, tiled=True)  33.7 us
    pallas_call x7, Pallas kernels, run(): pl.pallas_call(kernel, out_shape=out, in_specs=[HBM] * far + [VMEM] * (le...  10.6 us
    all_to_all x1, waiting for transfers between devices, on_device(): lax.all_to_all(away, 'tile', split_axis=0, concat_axis=0, tiled=True)  4.94 us
    all_to_all x1, starting transfers between devices, on_device(): lax.all_to_all(away, 'tile', split_axis=0, concat_axis=0, tiled=True)  3.53 us
    ppermute x2, waiting for transfers between devices, on_device(): partner = lax.ppermute(trace, 'mp', [(0, 1), (1, 0)])  1.93 us
  transfers between devices with their start and end apart: 3, of which 3 were waited for; matrix products, arithmetic and copies ran while one was open for 0% of the time, Pallas kernels for 4%

profile of v6, /device:TPU:0, one launch (start us, length us, event | category | flops | bytes accessed | tf_op | source)
XLA Modules:
  0.0 56.2 jit_solution(11629336422048362091)
XLA Ops:
  1.3 2.0 %prepare.1 = (bf16[16,80,128]{2,1,0:T(8,128)(2,1)S(1)}, f32[16,2,24,128]{3,2,1,0:T(8,128)S(1)}, f32[32,128]{1,0:T(8,128)S(1)}, f32[32,128]{1,0:T(8,128)S(1)}, f3...) custom-call(f32[1,4]{1,0:T(1,128)} %rates_far.1, f32[1,19]{1,0:T(1,128)} %vertical_far.1, ...), custom_call_target="tpu_custom_call" | custom-call | flops 1000000 | tf_op jit(solution)/shard_map/prepare/pallas_call | solution.py:30
  3.3 19.5 %all_to_all.15.refs_2_ = bf16[16,80,128]{2,1,0:T(8,128)(2,1)S(1)} all-to-all(bf16[16,80,128]{2,1,0:T(8,128)(2,1)S(1)} %get-tuple-element.16), channel_id=1, replica_groups=mesh['mp'=2,'tile'=16] {'tile'}, dimensions={0} | all-to-all | bytes 655360 | tf_op jit(solution)/shard_map/all_to_all | solution.py:460
  22.7 1.8 %evolve.2 = (f32[2,64,128]{2,1,0:T(8,128)S(1)}, bf16[16,24,256]{2,1,0:T(8,128)(2,1)S(1)}, bf16[8,256,256]{2,1,0:T(8,128)(2,1)S(1)}) custom-call(bf16[16,256,256]{2,1,0:T(8,128)(2,1)} %bitcast.13, f32[32,128]{1,0:T(8,128)S(1)} %get-tuple-element.15.refs_1_.refs_0_, bf16[16,80,128]{2,1,0:T(8,128)(2,1)S(1)} %all_to_all.15.refs_2_), custom_call_target="tpu_custom_call" | custom-call | flops 1000000 | tf_op jit(solution)/shard_map/evolve/pallas_call | solution.py:30
  24.5 0.1 collective-permute-start
  24.6 1.4 %collective-permute-done.trace = bf16[16,24,256]{2,1,0:T(8,128)(2,1)S(1)} collective-permute-done((bf16[16,24,256]{2,1,0:T(8,128)(2,1)S(1)}, bf16[16,24,256]{2,1,0:T(8,128)(2,1)S(1)}, u32[]{:S(2)}, u32[]{:S(2)}) %collective-permute-start) | collective-permute-done | bytes 196640 | tf_op jit(solution)/shard_map/ppermute | solution.py:477
  26.0 0.0 copy-start
  26.0 0.8 %redrive.1 = bf16[16,72,128]{2,1,0:T(8,128)(2,1)S(1)} custom-call(bf16[16,24,256]{2,1,0:T(8,128)(2,1)S(1)} %collective-permute-done.trace, bf16[8,256,256]{2,1,0:T(8,128)(2,1)S(1)} %get-tuple-element.18.lower, bf16[8,256,256]{2,1,0:T(8,128)(2,1)S(1)} %get-tuple-element.19.upper, f32[16,2,24,128]{3,2,1,0:T(8,128)S(1)} %get-tuple-element.20.base, ...), custom_call_target="tpu_custom_call" | custom-call | flops 1000000 | tf_op jit(solution)/shard_map/redrive/pallas_call | solution.py:30
  26.8 14.3 %all_to_all.16.refs_1_ = bf16[16,72,128]{2,1,0:T(8,128)(2,1)S(1)} all-to-all(bf16[16,72,128]{2,1,0:T(8,128)(2,1)S(1)} %redrive.1), channel_id=1, replica_groups=mesh['mp'=2,'tile'=16] {'tile'}, dimensions={0} | all-to-all | bytes 589824 | tf_op jit(solution)/shard_map/all_to_all | solution.py:460
  41.1 2.5 %evolve.3 = (bf16[16,24,256]{2,1,0:T(8,128)(2,1)S(1)}, bf16[16,24,256]{2,1,0:T(8,128)(2,1)}) custom-call(f32[32,128]{1,0:T(8,128)S(1)} %get-tuple-element.15.refs_1_.refs_0_, bf16[16,72,128]{2,1,0:T(8,128)(2,1)S(1)} %all_to_all.16.refs_1_, f32[2,64,128]{2,1,0:T(8,128)S(1)} %get-tuple-element.22.refs_2_), custom_call_target="tpu_custom_call" | custom-call | flops 1000000 | tf_op jit(solution)/shard_map/evolve/pallas_call | solution.py:30
  43.6 3.5 %all-to-all-start.2 = ((bf16[16,24,256]{2,1,0:T(8,128)(2,1)}), bf16[16,24,256]{2,1,0:T(8,128)(2,1)S(1)}, u32[]{:S(2)}, u32[]{:S(2)}) async-start(bf16[16,24,256]{2,1,0:T(8,128)(2,1)} %get-tuple-element.23), calls=%async_computation.2 | async-start | bytes 393216 | tf_op jit(solution)/shard_map/all_to_all | solution.py:485
  47.1 0.1 collective-permute-start.1
  47.2 0.0 copy-done
  47.2 0.9 %unforced.1 = (f32[20,4,1024]{2,1,0:T(4,128)S(1)}, bf16[72,128]{1,0:T(8,128)(2,1)S(1)}) custom-call(f32[20,4,1024]{2,1,0:T(4,128)S(1)} %bitcast.11, f32[25,24,128]{2,1,0:T(8,128)S(1)} %get-tuple-element.24.powers), custom_call_target="tpu_custom_call" | custom-call | flops 1000000 | tf_op jit(solution)/shard_map/unforced/pallas_call | solution.py:30
  48.1 0.5 collective-permute-done.1.trace
  48.6 1.6 %remap.1 = f32[24,4,1024]{2,1,0:T(4,128)} custom-call(bf16[16,24,256]{2,1,0:T(8,128)(2,1)S(1)} %collective-permute-done.1.trace, bf16[8,256,256]{2,1,0:T(8,128)(2,1)S(1)} %get-tuple-element.18.lower, bf16[8,256,256]{2,1,0:T(8,128)(2,1)S(1)} %get-tuple-element.19.upper), custom_call_target="tpu_custom_call" | custom-call | flops 1000000 | tf_op jit(solution)/shard_map/remap/pallas_call | solution.py:30
  50.2 4.9 %all-to-all-done.2.history = bf16[16,24,256]{2,1,0:T(8,128)(2,1)S(1)} async-done(((bf16[16,24,256]{2,1,0:T(8,128)(2,1)}), bf16[16,24,256]{2,1,0:T(8,128)(2,1)S(1)}, u32[]{:S(2)}, u32[]{:S(2)}) %all-to-all-start.2) | async-done | bytes 196640 | tf_op jit(solution)/shard_map/all_to_all | solution.py:485
  55.1 1.1 %finish.1 = f32[20,4,1024]{2,1,0:T(4,128)} custom-call(bf16[16,24,256]{2,1,0:T(8,128)(2,1)S(1)} %all-to-all-done.2.history, f32[20,4,1024]{2,1,0:T(4,128)S(1)} %get-tuple-element.25.rest, bf16[72,128]{1,0:T(8,128)(2,1)S(1)} %get-tuple-element.26.stack), custom_call_target="tpu_custom_call" | custom-call | flops 1000000 | tf_op jit(solution)/shard_map/finish/pallas_call | solution.py:30
Async XLA Ops:
  24.5 1.5 %collective-permute-start = (bf16[16,24,256]{2,1,0:T(8,128)(2,1)S(1)}, bf16[16,24,256]{2,1,0:T(8,128)(2,1)S(1)}, u32[]{:S(2)}, u32[]{:S(2)}) collective-permute-start(bf16[16,24,256]{2,1,0:T(8,128)(2,1)S(1)} %get-tuple-element.17), channel_id=1, source_target_pairs={{0,16},{16,0},{1,17},{17,1},{2,18},{18,2},{3,19},{19,3},{4,20},{20... | collective-permute-start | bytes 589832 | tf_op jit(solution)/shard_map/ppermute | solution.py:477
  26.0 21.2 %copy-start = (f32[1,20,4,1024]{3,2,1,0:T(4,128)S(1)}, f32[1,20,4,1024]{3,2,1,0:T(4,128)}, u32[]{:S(2)}) copy-start(f32[1,20,4,1024]{3,2,1,0:T(4,128)} %param.9) | copy-start | bytes 983044
  43.6 11.6 %all-to-all-start.2 = ((bf16[16,24,256]{2,1,0:T(8,128)(2,1)}), bf16[16,24,256]{2,1,0:T(8,128)(2,1)S(1)}, u32[]{:S(2)}, u32[]{:S(2)}) async-start(bf16[16,24,256]{2,1,0:T(8,128)(2,1)} %get-tuple-element.23), calls=%async_computation.2 | async-start | bytes 393216 | tf_op jit(solution)/shard_map/all_to_all | solution.py:485
  47.1 1.5 %collective-permute-start.1 = (bf16[16,24,256]{2,1,0:T(8,128)(2,1)S(1)}, bf16[16,24,256]{2,1,0:T(8,128)(2,1)S(1)}, u32[]{:S(2)}, u32[]{:S(2)}) collective-permute-start(bf16[16,24,256]{2,1,0:T(8,128)(2,1)S(1)} %get-tuple-element.27), channel_id=1, source_target_pairs={{0,16},{16,0},{1,17},{17,1},{2,18},{18,2},{3,19},{19,3},{4,20},{20... | collective-permute-start | bytes 589832 | tf_op jit(solution)/shard_map/ppermute | solution.py:477
